TPU v7x, 64 devices: a 2x2x8 block of a 4x4x8 slice. The times are simulated.
64 devices in a mesh: dp: 4 (over x, y), cp: 16 (over z, core).
Axes of the slice: x: 2, y: 2, z: 8, core: 2. Of those that a mesh axis runs over, the one named last changes fastest.
The devices are a block of a 4x4x8 slice.
Arguments:
- x: bfloat16 [32768, 2560], P(('dp', 'cp')), parts along dimension 0
- g: bfloat16 [6, 2560], replicated
- wq: bfloat16 [6, 2560, 8, 256], replicated
- wk: bfloat16 [6, 2560, 4, 256], replicated
- wv: bfloat16 [6, 2560, 4, 256], replicated
- wo: bfloat16 [6, 8, 256, 2560], replicated
Outputs:
- output: bfloat16 [32768, 2560], P(('dp', 'cp')), parts along dimension 0
There are 4 independent parts. A program takes and returns all parts, laid end to end along the dimension named above; an argument that names none is the same for every part.
All inputs are finite; a program needn't handle non-finite values.
Results may differ from a plain program's by a relative error of at most 0.02.
Values are sent between devices in bfloat16 or wider.
A program may use at most 768 MiB of HBM per device.

v0:
```python
import jax
import jax.numpy as jnp
from jax import lax
from jax.sharding import PartitionSpec as P

W = 1024
EPS = 1e-6


def _rms(x, g):
    xf = x.astype(jnp.float32)
    n = xf * lax.rsqrt(jnp.mean(xf * xf, axis=-1, keepdims=True) + EPS)
    return (n * g.astype(jnp.float32)).astype(jnp.bfloat16)


def _attend(q, k, v, qp, kp, local):
    s = jnp.einsum('qhgd,khd->hgqk', q, k, preferred_element_type=jnp.float32) * q.shape[-1] ** -0.5
    ok = (kp[None, :] <= qp[:, None]) & (kp[None, :] >= 0)
    if local:
        ok = ok & (kp[None, :] > qp[:, None] - W)
    s = jnp.where(ok, s, -jnp.inf)
    p = jax.nn.softmax(s, axis=-1).astype(jnp.bfloat16)
    return jnp.einsum('hgqk,khd->qhgd', p, v, preferred_element_type=jnp.float32).astype(jnp.bfloat16)


def _local_run(q, k, v, qp, kp, qb):
    ds = lax.dynamic_slice_in_dim

    def blk(t0):
        return _attend(ds(q, t0, qb), ds(k, t0, W + qb), ds(v, t0, W + qb), ds(qp, t0, qb), ds(kp, t0, W + qb), True)

    return lax.map(blk, jnp.arange(q.shape[0] // qb) * qb).reshape(q.shape)


def _global(q, k, v, qp, kp, qb):
    nb = q.shape[0] // qb
    o = lax.map(lambda a: _attend(a[0], k, v, a[1], kp, False),
                (q.reshape((nb, qb) + q.shape[1:]), qp.reshape(nb, qb)))
    return o.reshape(q.shape)


def _proj(n, w):
    y = jnp.dot(n, w.reshape(n.shape[-1], -1), preferred_element_type=jnp.float32).astype(jnp.bfloat16)
    return y.reshape((n.shape[0],) + w.shape[1:])


def solution(mesh):
    cp = mesh.shape['cp']
    fwd = [(j, j + 1) for j in range(cp - 1)]
    bwd = [(j + 1, j) for j in range(cp - 1)]

    def body(x, g, wq, wk, wv, wo):
        t, d = x.shape
        r = t // 2
        hq, dh = wq.shape[2], wq.shape[3]
        value_a3 = wk.shape[2]
        qb = min(256, r)
        reach = -(-W // r)
        i = lax.axis_index('cp')
        ar = jnp.arange(r)
        runs = jnp.stack([i, 2 * cp - 1 - i])
        pos = (runs[:, None] * r + ar).reshape(-1)
        dev = jnp.arange(cp)
        allpos = (jnp.stack([dev, 2 * cp - 1 - dev], axis=1)[:, :, None] * r + ar).reshape(-1)
        win = jnp.arange(W + r) - W
        nl = g.shape[0]
        for l in range(nl):
            n = _rms(x, g[l])
            q = _proj(n, wq[l]).reshape(t, value_a3, hq // value_a3, dh)
            kv = jnp.stack([_proj(n, wk[l]), _proj(n, wv[l])])
            if l < nl - 1:
                blk_a, blk_b = kv[:, :r], kv[:, r:]
                got_a, got_b = [], []
                for h in range(reach):
                    need = min(r, W - h * r)
                    send_a = blk_a[:, blk_a.shape[1] - need:]
                    send_b = blk_b[:, blk_b.shape[1] - need:]
                    blk_a = lax.ppermute(send_a, 'cp', fwd)
                    blk_b = jnp.where(i == cp - 1, send_a, lax.ppermute(send_b, 'cp', bwd))
                    got_a.insert(0, blk_a)
                    got_b.insert(0, blk_b)
                ka = jnp.concatenate(got_a + [kv[:, :r]], axis=1)
                kb = jnp.concatenate(got_b + [kv[:, r:]], axis=1)
                oa = _local_run(q[:r], ka[0], ka[1], pos[:r], runs[0] * r + win, qb)
                ob = _local_run(q[r:], kb[0], kb[1], pos[r:], runs[1] * r + win, qb)
                o = jnp.concatenate([oa, ob])
            else:
                kvg = lax.all_gather(kv, 'cp', axis=1, tiled=True)
                o = _global(q, kvg[0], kvg[1], pos, allpos, qb)
            y = jnp.dot(o.reshape(t, hq * dh), wo[l].reshape(hq * dh, d), preferred_element_type=jnp.float32)
            x = (x.astype(jnp.float32) + y).astype(jnp.bfloat16)
        return x

    spec = P(('dp', 'cp'), None)
    return jax.shard_map(body, mesh=mesh, in_specs=(spec, P(), P(), P(), P(), P()), out_specs=spec,
                         check_vma=False)
```

profile of v0, /device:TPU:21, one launch (start us, length us, event | category | flops | bytes accessed | tf_op | source)
XLA Modules:
  0.0 1576.9 jit_solution(16160290885436022809)
XLA Ops:
  8.4 22.6 %fusion.247 = (bf16[1,2560,4,256]{3,2,1,0:T(4,128)(2,1)}, bf16[1,2560,4,256]{3,2,1,0:T(4,128)(2,1)}, bf16[1,2560,4,256]{3,2,1,0:T(4,128)(2,1)}, bf16[1,2560,4,25...) fusion(bf16[6,2560,4,256]{3,2,1,0:T(4,128)(2,1)} %param.11), kind=kLoop, calls=%fused_computation.400 | loop fusion | bytes 62914560 | tf_op jit(solution)/shard_map/slice | solution.py:70
  37.2 23.0 %fusion.248 = (bf16[1,2560,4,256]{3,2,1,0:T(4,128)(2,1)}, bf16[1,2560,4,256]{3,2,1,0:T(4,128)(2,1)}, bf16[1,2560,4,256]{3,2,1,0:T(4,128)(2,1)}, bf16[1,2560,4,25...) fusion(bf16[6,2560,4,256]{3,2,1,0:T(4,128)(2,1)} %param.12), kind=kLoop, calls=%fused_computation.401 | loop fusion | bytes 62914560 | tf_op jit(solution)/shard_map/slice | solution.py:70
  77.9 41.7 %fusion.245 = (bf16[1,8,256,2560]{3,2,1,0:T(8,128)(2,1)}, bf16[1,8,256,2560]{3,2,1,0:T(8,128)(2,1)}, bf16[1,8,256,2560]{3,2,1,0:T(8,128)(2,1)}, bf16[1,8,256,256...) fusion(bf16[6,8,256,2560]{3,2,1,0:T(8,128)(2,1)} %param.13), kind=kLoop, calls=%fused_computation.398 | loop fusion | bytes 125829120 | tf_op jit(solution)/shard_map/slice | solution.py:90
  121.6 41.0 %fusion.246 = (bf16[1,2560,8,256]{3,2,1,0:T(8,128)(2,1)}, bf16[1,2560,8,256]{3,2,1,0:T(8,128)(2,1)}, bf16[1,2560,8,256]{3,2,1,0:T(8,128)(2,1)}, bf16[1,2560,8,25...) fusion(bf16[6,2560,8,256]{3,2,1,0:T(8,128)(2,1)} %param.10), kind=kLoop, calls=%fused_computation.399 | loop fusion | bytes 125829120 | tf_op jit(solution)/shard_map/slice | solution.py:69
  162.5 12.6 copy.259
  177.4 10.4 convolution_convert_fusion.5
  195.1 10.2 collective-permute-done.3
  215.4 12.5 collective-permute-done.5
  259.7 8.7 fusion.140
  282.7 8.7 fusion.139
  291.5 9.6 fusion.46
  318.4 14.2 collective-permute-done.12
  335.7 11.7 collective-permute-done.8
  351.8 11.7 collective-permute-done.9
  368.2 12.6 copy.262
  440.9 8.7 fusion.138
  472.4 10.8 fusion.50
  500.6 14.2 collective-permute-done.20
  517.8 11.7 collective-permute-done.16
  534.0 11.7 collective-permute-done.17
  550.3 12.5 copy.265
  622.9 8.6 fusion.136
  654.3 10.8 fusion.54
  682.5 14.2 collective-permute-done.28
  699.8 11.7 collective-permute-done.24
  715.9 11.7 collective-permute-done.25
  732.2 12.6 copy.268
  807.5 8.7 fusion.134
  839.0 10.8 fusion.58
  867.1 14.2 collective-permute-done.36
  884.4 11.7 collective-permute-done.32
  900.6 11.7 collective-permute-done.33
  916.9 12.5 copy.271
  944.9 10.4 collective-permute-start.35
  996.3 8.7 fusion.132
  1027.7 10.8 fusion.62
  1055.4 12.5 copy.272
  1068.7 9.2 convolution_convert_fusion
  1080.7 170.2 %all-gather.2.cloned.1.call-done = bf16[2,8192,4,256]{3,1,2,0:T(8,128)(2,1)} async-done(((bf16[2,512,4,256]{3,1,2,0:T(8,128)(2,1)}), bf16[2,8192,4,256]{3,1,2,0:T(8,128)(2,1)}) %all-gather.2.cloned.1.call-update) | async-done | bytes 33554448 | tf_op jit(solution)/shard_map/all_gather | solution.py:88
  1250.9 22.7 %slice_bitcast_fusion = (bf16[8192,4,256]{2,0,1:T(8,128)(2,1)}, bf16[8192,4,256]{2,0,1:T(8,128)(2,1)}) fusion(bf16[2,8192,4,256]{3,1,2,0:T(8,128)(2,1)} %all-gather.2.cloned.1.call-done), kind=kLoop, calls=%fused_computation.36 | loop fusion | bytes 67108864 | tf_op jit(solution)/shard_map/squeeze | solution.py:89
  1273.5 281.5 %while.3 = (s32[]{:T(128)}, bf16[2,256,4,2,256]{4,3,2,1,0:T(2,128)(2,1)}, s32[2,256]{1,0:T(2,128)}, bf16[2,256,4,2,256]{4,3,2,1,0:T(2,128)(2,1)}, bf16[8192,4,25...) while((s32[]{:T(128)}, ...), condition=%wide.region_29.30_spmd.clone, body=%wide.region_26.29_spmd.clone.sunk | while | flops 17318830080 | bytes 329452832 | solution.py:37
  1278.7 33.3 %fusion.298 = f32[4,256,2,8192]{3,1,2,0:T(8,128)} fusion(bf16[8192,4,256]{2,0,1:T(8,128)(2,1)} %get-tuple-element.455, bf16[1,256,4,2,256]{4,3,2,1,0:T(2,128)(2,1)S(1)} %constant_dynamic-slice_fusion.4), kind=kOutput, calls=%fused_computation.13.clone.1 | convolution fusion | flops 8589934592 | bytes 84934656 | tf_op jit(solution)/shard_map/while/body/eval_jaxpr/qhgd,khd->hgqk/dot_general | solution.py:17
  1312.0 72.2 %fusion.299 = (f32[4,2,256]{2,1,0:T(2,128)S(1)}, f32[4,2,256,8192]{3,2,1,0:T(8,128)}) fusion(f32[4,256,2,8192]{3,1,2,0:T(8,128)} %fusion.298, pred[256,8192]{1,0:T(8,128)(4,1)S(1)} %compare_and_fusion.4), kind=kOutput, calls=%fused_computation.397.clone.1 | output fusion | flops 100671488 | bytes 136323072 | tf_op jit(solution)/shard_map/while/body/eval_jaxpr/sub | solution.py:22
  1384.2 27.7 %fusion.300 = bf16[1,256,4,2,256]{4,1,3,2,0:T(8,128)(2,1)S(1)} fusion(bf16[8192,4,256]{2,0,1:T(8,128)(2,1)} %get-tuple-element.456, f32[4,2,256,8192]{3,2,1,0:T(8,128)} %get-tuple-element.433, f32[4,2,256]{2,1,0:T(2,128)S(1)} %get-tuple-element.434), kind=kOutput, calls=%fused_computation.17.clone.1 | convolution fusion | flops 8624013312 | bytes 84942848 | tf_op jit(solution)/shard_map/while/body/eval_jaxpr/hgqk,khd->qhgd/dot_general | solution.py:23
  1419.3 33.3 %fusion.298 = f32[4,256,2,8192]{3,1,2,0:T(8,128)} fusion(bf16[8192,4,256]{2,0,1:T(8,128)(2,1)} %get-tuple-element.455, bf16[1,256,4,2,256]{4,3,2,1,0:T(2,128)(2,1)S(1)} %constant_dynamic-slice_fusion.4), kind=kOutput, calls=%fused_computation.13.clone.1 | convolution fusion | flops 8589934592 | bytes 84934656 | tf_op jit(solution)/shard_map/while/body/eval_jaxpr/qhgd,khd->hgqk/dot_general | solution.py:17
  1452.6 72.2 %fusion.299 = (f32[4,2,256]{2,1,0:T(2,128)S(1)}, f32[4,2,256,8192]{3,2,1,0:T(8,128)}) fusion(f32[4,256,2,8192]{3,1,2,0:T(8,128)} %fusion.298, pred[256,8192]{1,0:T(8,128)(4,1)S(1)} %compare_and_fusion.4), kind=kOutput, calls=%fused_computation.397.clone.1 | output fusion | flops 100671488 | bytes 136323072 | tf_op jit(solution)/shard_map/while/body/eval_jaxpr/sub | solution.py:22
  1524.8 27.7 %fusion.300 = bf16[1,256,4,2,256]{4,1,3,2,0:T(8,128)(2,1)S(1)} fusion(bf16[8192,4,256]{2,0,1:T(8,128)(2,1)} %get-tuple-element.456, f32[4,2,256,8192]{3,2,1,0:T(8,128)} %get-tuple-element.433, f32[4,2,256]{2,1,0:T(2,128)S(1)} %get-tuple-element.434), kind=kOutput, calls=%fused_computation.17.clone.1 | convolution fusion | flops 8624013312 | bytes 84942848 | tf_op jit(solution)/shard_map/while/body/eval_jaxpr/hgqk,khd->qhgd/dot_general | solution.py:23
  1558.3 11.2 fusion.65
  (467 shorter events, 578.8 us)
Async XLA Ops:
  6.5 1244.3 %all-gather.2.cloned.1.call-start = ((), (), s32[]{:S(2)}) async-start(), calls=%async_computation | async-start | bytes 35651584 | tf_op jit(solution)/shard_map/all_gather | solution.py:88
  69.0 50.5 %collective-permute-start = (bf16[2,256,4,256]{3,1,2,0:T(8,128)(2,1)S(1)}, bf16[2,256,4,256]{3,1,2,0:T(8,128)(2,1)}, u32[]{:S(2)}, u32[]{:S(2)}) collective-permute-start(bf16[2,256,4,256]{3,1,2,0:T(8,128)(2,1)S(1)} %get-tuple-element.367), channel_id=1, source_target_pairs={{0,1},{1,2},{2,3},{3,4},{4,5},{5,6},{6,7},{7,8},{8,9},{9,10},{10,1... | collective-permute-start | bytes 3145736 | tf_op jit(solution)/shard_map/ppermute | solution.py:78
  74.1 135.3 %collective-permute-start.4 = (bf16[2,256,4,256]{3,1,2,0:T(8,128)(2,1)}, bf16[2,256,4,256]{3,1,2,0:T(8,128)(2,1)}, u32[]{:S(2)}, u32[]{:S(2)}) collective-permute-start(bf16[2,256,4,256]{3,1,2,0:T(8,128)(2,1)} %get-tuple-element.366), channel_id=1, source_target_pairs={{1,0},{2,1},{3,2},{4,3},{5,4},{6,5},{7,6},{8,7},{9,8},{10,9},{11,1... | collective-permute-start | bytes 3145736 | tf_op jit(solution)/shard_map/ppermute | solution.py:79
  119.6 55.5 %collective-permute-start.1 = (bf16[2,256,4,256]{3,1,2,0:T(8,128)(2,1)}, bf16[2,256,4,256]{3,1,2,0:T(8,128)(2,1)S(1)}, u32[]{:S(2)}, u32[]{:S(2)}) collective-permute-start(bf16[2,256,4,256]{3,1,2,0:T(8,128)(2,1)} %collective-permute-done), channel_id=1, source_target_pairs={{0,1},{1,2},{2,3},{3,4},{4,5},{5,6},{6,7},{7,8},{8,9},{9,10},{10,1... | collective-permute-start | bytes 3145736 | tf_op jit(solution)/shard_map/ppermute | solution.py:78
  175.1 32.9 %copy-start.18 = (bf16[2,256,4,256]{3,1,2,0:T(8,128)(2,1)}, bf16[2,256,4,256]{3,1,2,0:T(8,128)(2,1)S(1)}, u32[]{:S(2)}) copy-start(bf16[2,256,4,256]{3,1,2,0:T(8,128)(2,1)S(1)} %collective-permute-done.1) | copy-start | bytes 3145732
  175.1 14.0 collective-permute-start.2
  189.2 16.1 %collective-permute-start.3 = (bf16[2,256,4,256]{3,1,2,0:T(8,128)(2,1)}, bf16[2,256,4,256]{3,1,2,0:T(8,128)(2,1)}, u32[]{:S(2)}, u32[]{:S(2)}) collective-permute-start(bf16[2,256,4,256]{3,1,2,0:T(8,128)(2,1)} %collective-permute-done.2), channel_id=1, source_target_pairs={{0,1},{1,2},{2,3},{3,4},{4,5},{5,6},{6,7},{7,8},{8,9},{9,10},{10,1... | collective-permute-start | bytes 3145736 | tf_op jit(solution)/shard_map/ppermute | solution.py:78
  211.1 16.9 %collective-permute-start.5 = (bf16[2,256,4,256]{3,1,2,0:T(8,128)(2,1)S(1)}, bf16[2,256,4,256]{3,1,2,0:T(8,128)(2,1)S(1)}, u32[]{:S(2)}, u32[]{:S(2)}) collective-permute-start(bf16[2,256,4,256]{3,1,2,0:T(8,128)(2,1)S(1)} %get-tuple-element.365), channel_id=1, source_target_pairs={{1,0},{2,1},{3,2},{4,3},{5,4},{6,5},{7,6},{8,7},{9,8},{10,9},{11,1... | collective-permute-start | bytes 3145736 | tf_op jit(solution)/shard_map/ppermute | solution.py:79
  229.1 23.0 %collective-permute-start.6 = (bf16[2,256,4,256]{3,1,2,0:T(8,128)(2,1)}, bf16[2,256,4,256]{3,1,2,0:T(8,128)(2,1)}, u32[]{:S(2)}, u32[]{:S(2)}) collective-permute-start(bf16[2,256,4,256]{3,1,2,0:T(8,128)(2,1)} %broadcast_select_fusion.13), channel_id=1, source_target_pairs={{1,0},{2,1},{3,2},{4,3},{5,4},{6,5},{7,6},{8,7},{9,8},{10,9},{11,1... | collective-permute-start | bytes 3145736 | tf_op jit(solution)/shard_map/ppermute | solution.py:79
  254.2 16.1 %collective-permute-start.7 = (bf16[2,256,4,256]{3,1,2,0:T(8,128)(2,1)S(1)}, bf16[2,256,4,256]{3,1,2,0:T(8,128)(2,1)}, u32[]{:S(2)}, u32[]{:S(2)}) collective-permute-start(bf16[2,256,4,256]{3,1,2,0:T(8,128)(2,1)S(1)} %broadcast_select_fusion.12), channel_id=1, source_target_pairs={{1,0},{2,1},{3,2},{4,3},{5,4},{6,5},{7,6},{8,7},{9,8},{10,9},{11,1... | collective-permute-start | bytes 3145736 | tf_op jit(solution)/shard_map/ppermute | solution.py:79
  316.4 16.1 %collective-permute-start.12 = (bf16[2,256,4,256]{3,1,2,0:T(8,128)(2,1)S(1)}, bf16[2,256,4,256]{3,1,2,0:T(8,128)(2,1)S(1)}, u32[]{:S(2)}, u32[]{:S(2)}) collective-permute-start(bf16[2,256,4,256]{3,1,2,0:T(8,128)(2,1)S(1)} %pad_maximum_fusion.4), channel_id=1, source_target_pairs={{1,0},{2,1},{3,2},{4,3},{5,4},{6,5},{7,6},{8,7},{9,8},{10,9},{11,1... | collective-permute-start | bytes 3145736 | tf_op jit(solution)/shard_map/ppermute | solution.py:79
  333.7 13.6 collective-permute-start.8
  347.4 16.1 %collective-permute-start.9 = (bf16[2,256,4,256]{3,1,2,0:T(8,128)(2,1)S(1)}, bf16[2,256,4,256]{3,1,2,0:T(8,128)(2,1)}, u32[]{:S(2)}, u32[]{:S(2)}) collective-permute-start(bf16[2,256,4,256]{3,1,2,0:T(8,128)(2,1)S(1)} %collective-permute-done.8), channel_id=1, source_target_pairs={{0,1},{1,2},{2,3},{3,4},{4,5},{5,6},{6,7},{7,8},{8,9},{9,10},{10,1... | collective-permute-start | bytes 3145736 | tf_op jit(solution)/shard_map/ppermute | solution.py:78
  363.5 32.7 %collective-permute-start.10 = (bf16[2,256,4,256]{3,1,2,0:T(8,128)(2,1)}, bf16[2,256,4,256]{3,1,2,0:T(8,128)(2,1)S(1)}, u32[]{:S(2)}, u32[]{:S(2)}) collective-permute-start(bf16[2,256,4,256]{3,1,2,0:T(8,128)(2,1)} %collective-permute-done.9), channel_id=1, source_target_pairs={{0,1},{1,2},{2,3},{3,4},{4,5},{5,6},{6,7},{7,8},{8,9},{9,10},{10,1... | collective-permute-start | bytes 3145736 | tf_op jit(solution)/shard_map/ppermute | solution.py:78
  394.2 18.8 %collective-permute-start.13 = (bf16[2,256,4,256]{3,1,2,0:T(8,128)(2,1)S(1)}, bf16[2,256,4,256]{3,1,2,0:T(8,128)(2,1)S(1)}, u32[]{:S(2)}, u32[]{:S(2)}) collective-permute-start(bf16[2,256,4,256]{3,1,2,0:T(8,128)(2,1)S(1)} %copy-done.26), channel_id=1, source_target_pairs={{1,0},{2,1},{3,2},{4,3},{5,4},{6,5},{7,6},{8,7},{9,8},{10,9},{11,1... | collective-permute-start | bytes 3145736 | tf_op jit(solution)/shard_map/ppermute | solution.py:79
  396.2 15.4 collective-permute-start.11
  415.8 16.9 %collective-permute-start.14 = (bf16[2,256,4,256]{3,1,2,0:T(8,128)(2,1)S(1)}, bf16[2,256,4,256]{3,1,2,0:T(8,128)(2,1)}, u32[]{:S(2)}, u32[]{:S(2)}) collective-permute-start(bf16[2,256,4,256]{3,1,2,0:T(8,128)(2,1)S(1)} %get-tuple-element.375), channel_id=1, source_target_pairs={{1,0},{2,1},{3,2},{4,3},{5,4},{6,5},{7,6},{8,7},{9,8},{10,9},{11,1... | collective-permute-start | bytes 3145736 | tf_op jit(solution)/shard_map/ppermute | solution.py:79
  435.8 16.1 %collective-permute-start.15 = (bf16[2,256,4,256]{3,1,2,0:T(8,128)(2,1)}, bf16[2,256,4,256]{3,1,2,0:T(8,128)(2,1)}, u32[]{:S(2)}, u32[]{:S(2)}) collective-permute-start(bf16[2,256,4,256]{3,1,2,0:T(8,128)(2,1)} %broadcast_select_fusion.9), channel_id=1, source_target_pairs={{1,0},{2,1},{3,2},{4,3},{5,4},{6,5},{7,6},{8,7},{9,8},{10,9},{11,1... | collective-permute-start | bytes 3145736 | tf_op jit(solution)/shard_map/ppermute | solution.py:79
  498.6 16.1 %collective-permute-start.20 = (bf16[2,256,4,256]{3,1,2,0:T(8,128)(2,1)S(1)}, bf16[2,256,4,256]{3,1,2,0:T(8,128)(2,1)S(1)}, u32[]{:S(2)}, u32[]{:S(2)}) collective-permute-start(bf16[2,256,4,256]{3,1,2,0:T(8,128)(2,1)S(1)} %pad_maximum_fusion.3), channel_id=1, source_target_pairs={{1,0},{2,1},{3,2},{4,3},{5,4},{6,5},{7,6},{8,7},{9,8},{10,9},{11,1... | collective-permute-start | bytes 3145736 | tf_op jit(solution)/shard_map/ppermute | solution.py:79
  515.9 13.6 collective-permute-start.16
  529.5 16.1 %collective-permute-start.17 = (bf16[2,256,4,256]{3,1,2,0:T(8,128)(2,1)S(1)}, bf16[2,256,4,256]{3,1,2,0:T(8,128)(2,1)}, u32[]{:S(2)}, u32[]{:S(2)}) collective-permute-start(bf16[2,256,4,256]{3,1,2,0:T(8,128)(2,1)S(1)} %collective-permute-done.16), channel_id=1, source_target_pairs={{0,1},{1,2},{2,3},{3,4},{4,5},{5,6},{6,7},{7,8},{8,9},{9,10},{10,1... | collective-permute-start | bytes 3145736 | tf_op jit(solution)/shard_map/ppermute | solution.py:78
  545.7 32.6 %collective-permute-start.18 = (bf16[2,256,4,256]{3,1,2,0:T(8,128)(2,1)}, bf16[2,256,4,256]{3,1,2,0:T(8,128)(2,1)S(1)}, u32[]{:S(2)}, u32[]{:S(2)}) collective-permute-start(bf16[2,256,4,256]{3,1,2,0:T(8,128)(2,1)} %collective-permute-done.17), channel_id=1, source_target_pairs={{0,1},{1,2},{2,3},{3,4},{4,5},{5,6},{6,7},{7,8},{8,9},{9,10},{10,1... | collective-permute-start | bytes 3145736 | tf_op jit(solution)/shard_map/ppermute | solution.py:78
  576.3 18.8 %collective-permute-start.21 = (bf16[2,256,4,256]{3,1,2,0:T(8,128)(2,1)S(1)}, bf16[2,256,4,256]{3,1,2,0:T(8,128)(2,1)S(1)}, u32[]{:S(2)}, u32[]{:S(2)}) collective-permute-start(bf16[2,256,4,256]{3,1,2,0:T(8,128)(2,1)S(1)} %copy-done.28), channel_id=1, source_target_pairs={{1,0},{2,1},{3,2},{4,3},{5,4},{6,5},{7,6},{8,7},{9,8},{10,9},{11,1... | collective-permute-start | bytes 3145736 | tf_op jit(solution)/shard_map/ppermute | solution.py:79
  578.3 15.4 collective-permute-start.19
  597.8 16.9 %collective-permute-start.22 = (bf16[2,256,4,256]{3,1,2,0:T(8,128)(2,1)S(1)}, bf16[2,256,4,256]{3,1,2,0:T(8,128)(2,1)}, u32[]{:S(2)}, u32[]{:S(2)}) collective-permute-start(bf16[2,256,4,256]{3,1,2,0:T(8,128)(2,1)S(1)} %get-tuple-element.373), channel_id=1, source_target_pairs={{1,0},{2,1},{3,2},{4,3},{5,4},{6,5},{7,6},{8,7},{9,8},{10,9},{11,1... | collective-permute-start | bytes 3145736 | tf_op jit(solution)/shard_map/ppermute | solution.py:79
  617.8 16.1 %collective-permute-start.23 = (bf16[2,256,4,256]{3,1,2,0:T(8,128)(2,1)}, bf16[2,256,4,256]{3,1,2,0:T(8,128)(2,1)}, u32[]{:S(2)}, u32[]{:S(2)}) collective-permute-start(bf16[2,256,4,256]{3,1,2,0:T(8,128)(2,1)} %broadcast_select_fusion.6), channel_id=1, source_target_pairs={{1,0},{2,1},{3,2},{4,3},{5,4},{6,5},{7,6},{8,7},{9,8},{10,9},{11,1... | collective-permute-start | bytes 3145736 | tf_op jit(solution)/shard_map/ppermute | solution.py:79
  680.5 16.1 %collective-permute-start.28 = (bf16[2,256,4,256]{3,1,2,0:T(8,128)(2,1)S(1)}, bf16[2,256,4,256]{3,1,2,0:T(8,128)(2,1)S(1)}, u32[]{:S(2)}, u32[]{:S(2)}) collective-permute-start(bf16[2,256,4,256]{3,1,2,0:T(8,128)(2,1)S(1)} %pad_maximum_fusion.2), channel_id=1, source_target_pairs={{1,0},{2,1},{3,2},{4,3},{5,4},{6,5},{7,6},{8,7},{9,8},{10,9},{11,1... | collective-permute-start | bytes 3145736 | tf_op jit(solution)/shard_map/ppermute | solution.py:79
  697.8 13.6 collective-permute-start.24
  711.5 16.1 %collective-permute-start.25 = (bf16[2,256,4,256]{3,1,2,0:T(8,128)(2,1)S(1)}, bf16[2,256,4,256]{3,1,2,0:T(8,128)(2,1)}, u32[]{:S(2)}, u32[]{:S(2)}) collective-permute-start(bf16[2,256,4,256]{3,1,2,0:T(8,128)(2,1)S(1)} %collective-permute-done.24), channel_id=1, source_target_pairs={{0,1},{1,2},{2,3},{3,4},{4,5},{5,6},{6,7},{7,8},{8,9},{9,10},{10,1... | collective-permute-start | bytes 3145736 | tf_op jit(solution)/shard_map/ppermute | solution.py:78
  727.6 32.6 %collective-permute-start.26 = (bf16[2,256,4,256]{3,1,2,0:T(8,128)(2,1)}, bf16[2,256,4,256]{3,1,2,0:T(8,128)(2,1)S(1)}, u32[]{:S(2)}, u32[]{:S(2)}) collective-permute-start(bf16[2,256,4,256]{3,1,2,0:T(8,128)(2,1)} %collective-permute-done.25), channel_id=1, source_target_pairs={{0,1},{1,2},{2,3},{3,4},{4,5},{5,6},{6,7},{7,8},{8,9},{9,10},{10,1... | collective-permute-start | bytes 3145736 | tf_op jit(solution)/shard_map/ppermute | solution.py:78
  744.8 21.6 %slice-start.12 = ((s8[10485760]{0:T(1024)(128)(4,1)}), s8[4194304]{0:T(1024)(128)(4,1)S(1)}, s32[]{:S(2)}) async-start(s8[10485760]{0:T(1024)(128)(4,1)} %bitcast.472), calls=%async_computation.13 | async-start | bytes 8388608
  758.2 21.4 %collective-permute-start.29 = (bf16[2,256,4,256]{3,1,2,0:T(8,128)(2,1)S(1)}, bf16[2,256,4,256]{3,1,2,0:T(8,128)(2,1)S(1)}, u32[]{:S(2)}, u32[]{:S(2)}) collective-permute-start(bf16[2,256,4,256]{3,1,2,0:T(8,128)(2,1)S(1)} %copy-done.30), channel_id=1, source_target_pairs={{1,0},{2,1},{3,2},{4,3},{5,4},{6,5},{7,6},{8,7},{9,8},{10,9},{11,1... | collective-permute-start | bytes 3145736 | tf_op jit(solution)/shard_map/ppermute | solution.py:79
  760.2 18.0 %collective-permute-start.27 = (bf16[2,256,4,256]{3,1,2,0:T(8,128)(2,1)S(1)}, bf16[2,256,4,256]{3,1,2,0:T(8,128)(2,1)S(1)}, u32[]{:S(2)}, u32[]{:S(2)}) collective-permute-start(bf16[2,256,4,256]{3,1,2,0:T(8,128)(2,1)S(1)} %collective-permute-done.26), channel_id=1, source_target_pairs={{0,1},{1,2},{2,3},{3,4},{4,5},{5,6},{6,7},{7,8},{8,9},{9,10},{10,1... | collective-permute-start | bytes 3145736 | tf_op jit(solution)/shard_map/ppermute | solution.py:78
  782.3 16.9 %collective-permute-start.30 = (bf16[2,256,4,256]{3,1,2,0:T(8,128)(2,1)S(1)}, bf16[2,256,4,256]{3,1,2,0:T(8,128)(2,1)}, u32[]{:S(2)}, u32[]{:S(2)}) collective-permute-start(bf16[2,256,4,256]{3,1,2,0:T(8,128)(2,1)S(1)} %get-tuple-element.371), channel_id=1, source_target_pairs={{1,0},{2,1},{3,2},{4,3},{5,4},{6,5},{7,6},{8,7},{9,8},{10,9},{11,1... | collective-permute-start | bytes 3145736 | tf_op jit(solution)/shard_map/ppermute | solution.py:79
  802.4 16.1 %collective-permute-start.31 = (bf16[2,256,4,256]{3,1,2,0:T(8,128)(2,1)}, bf16[2,256,4,256]{3,1,2,0:T(8,128)(2,1)}, u32[]{:S(2)}, u32[]{:S(2)}) collective-permute-start(bf16[2,256,4,256]{3,1,2,0:T(8,128)(2,1)} %broadcast_select_fusion.3), channel_id=1, source_target_pairs={{1,0},{2,1},{3,2},{4,3},{5,4},{6,5},{7,6},{8,7},{9,8},{10,9},{11,1... | collective-permute-start | bytes 3145736 | tf_op jit(solution)/shard_map/ppermute | solution.py:79
  865.2 16.1 %collective-permute-start.36 = (bf16[2,256,4,256]{3,1,2,0:T(8,128)(2,1)S(1)}, bf16[2,256,4,256]{3,1,2,0:T(8,128)(2,1)S(1)}, u32[]{:S(2)}, u32[]{:S(2)}) collective-permute-start(bf16[2,256,4,256]{3,1,2,0:T(8,128)(2,1)S(1)} %pad_maximum_fusion.1), channel_id=1, source_target_pairs={{1,0},{2,1},{3,2},{4,3},{5,4},{6,5},{7,6},{8,7},{9,8},{10,9},{11,1... | collective-permute-start | bytes 3145736 | tf_op jit(solution)/shard_map/ppermute | solution.py:79
  882.5 13.6 collective-permute-start.32
  896.1 16.1 %collective-permute-start.33 = (bf16[2,256,4,256]{3,1,2,0:T(8,128)(2,1)S(1)}, bf16[2,256,4,256]{3,1,2,0:T(8,128)(2,1)}, u32[]{:S(2)}, u32[]{:S(2)}) collective-permute-start(bf16[2,256,4,256]{3,1,2,0:T(8,128)(2,1)S(1)} %collective-permute-done.32), channel_id=1, source_target_pairs={{0,1},{1,2},{2,3},{3,4},{4,5},{5,6},{6,7},{7,8},{8,9},{9,10},{10,1... | collective-permute-start | bytes 3145736 | tf_op jit(solution)/shard_map/ppermute | solution.py:78
  912.3 32.6 %collective-permute-start.34 = (bf16[2,256,4,256]{3,1,2,0:T(8,128)(2,1)}, bf16[2,256,4,256]{3,1,2,0:T(8,128)(2,1)S(1)}, u32[]{:S(2)}, u32[]{:S(2)}) collective-permute-start(bf16[2,256,4,256]{3,1,2,0:T(8,128)(2,1)} %collective-permute-done.33), channel_id=1, source_target_pairs={{0,1},{1,2},{2,3},{3,4},{4,5},{5,6},{6,7},{7,8},{8,9},{9,10},{10,1... | collective-permute-start | bytes 3145736 | tf_op jit(solution)/shard_map/ppermute | solution.py:78
  929.4 25.9 %slice-start.2 = ((s8[10485760]{0:T(1024)(128)(4,1)}), s8[4194304]{0:T(1024)(128)(4,1)S(1)}, s32[]{:S(2)}) async-start(s8[10485760]{0:T(1024)(128)(4,1)} %bitcast.463), calls=%async_computation.3 | async-start | bytes 8388608
  929.4 25.9 %slice-start.3 = ((s8[10485760]{0:T(1024)(128)(4,1)}), s8[4194304]{0:T(1024)(128)(4,1)S(1)}, s32[]{:S(2)}) async-start(s8[10485760]{0:T(1024)(128)(4,1)} %bitcast.463), calls=%async_computation.4 | async-start | bytes 8388608
  942.9 25.5 %collective-permute-start.37 = (bf16[2,256,4,256]{3,1,2,0:T(8,128)(2,1)S(1)}, bf16[2,256,4,256]{3,1,2,0:T(8,128)(2,1)S(1)}, u32[]{:S(2)}, u32[]{:S(2)}) collective-permute-start(bf16[2,256,4,256]{3,1,2,0:T(8,128)(2,1)S(1)} %copy-done.24), channel_id=1, source_target_pairs={{1,0},{2,1},{3,2},{4,3},{5,4},{6,5},{7,6},{8,7},{9,8},{10,9},{11,1... | collective-permute-start | bytes 3145736 | tf_op jit(solution)/shard_map/ppermute | solution.py:79
  944.9 22.2 %copy-start.20 = (bf16[2,256,4,256]{3,1,2,0:T(8,128)(2,1)}, bf16[2,256,4,256]{3,1,2,0:T(8,128)(2,1)S(1)}, u32[]{:S(2)}) copy-start(bf16[2,256,4,256]{3,1,2,0:T(8,128)(2,1)S(1)} %collective-permute-done.34) | copy-start | bytes 3145732
  944.9 22.1 %collective-permute-start.35 = (bf16[2,256,4,256]{3,1,2,0:T(8,128)(2,1)S(1)}, bf16[2,256,4,256]{3,1,2,0:T(8,128)(2,1)S(1)}, u32[]{:S(2)}, u32[]{:S(2)}) collective-permute-start(bf16[2,256,4,256]{3,1,2,0:T(8,128)(2,1)S(1)} %collective-permute-done.34), channel_id=1, source_target_pairs={{0,1},{1,2},{2,3},{3,4},{4,5},{5,6},{6,7},{7,8},{8,9},{9,10},{10,1... | collective-permute-start | bytes 3145736 | tf_op jit(solution)/shard_map/ppermute | solution.py:78
  971.1 16.9 %collective-permute-start.38 = (bf16[2,256,4,256]{3,1,2,0:T(8,128)(2,1)S(1)}, bf16[2,256,4,256]{3,1,2,0:T(8,128)(2,1)}, u32[]{:S(2)}, u32[]{:S(2)}) collective-permute-start(bf16[2,256,4,256]{3,1,2,0:T(8,128)(2,1)S(1)} %get-tuple-element.369), channel_id=1, source_target_pairs={{1,0},{2,1},{3,2},{4,3},{5,4},{6,5},{7,6},{8,7},{9,8},{10,9},{11,1... | collective-permute-start | bytes 3145736 | tf_op jit(solution)/shard_map/ppermute | solution.py:79
  991.2 16.1 %collective-permute-start.39 = (bf16[2,256,4,256]{3,1,2,0:T(8,128)(2,1)}, bf16[2,256,4,256]{3,1,2,0:T(8,128)(2,1)}, u32[]{:S(2)}, u32[]{:S(2)}) collective-permute-start(bf16[2,256,4,256]{3,1,2,0:T(8,128)(2,1)} %broadcast_select_fusion), channel_id=1, source_target_pairs={{1,0},{2,1},{3,2},{4,3},{5,4},{6,5},{7,6},{8,7},{9,8},{10,9},{11,1... | collective-permute-start | bytes 3145736 | tf_op jit(solution)/shard_map/ppermute | solution.py:79
  1384.2 27.7 %copy-start.50 = (bf16[2,256,4,2,256]{4,3,2,1,0:T(2,128)(2,1)S(1)}, bf16[2,256,4,2,256]{4,3,2,1,0:T(2,128)(2,1)}, u32[]{:S(2)}) copy-start(bf16[2,256,4,2,256]{4,3,2,1,0:T(2,128)(2,1)} %get-tuple-element.444) | copy-start | bytes 6291460 | tf_op jit(solution)/shard_map/while
  1524.8 27.7 %copy-start.50 = (bf16[2,256,4,2,256]{4,3,2,1,0:T(2,128)(2,1)S(1)}, bf16[2,256,4,2,256]{4,3,2,1,0:T(2,128)(2,1)}, u32[]{:S(2)}) copy-start(bf16[2,256,4,2,256]{4,3,2,1,0:T(2,128)(2,1)} %get-tuple-element.444) | copy-start | bytes 6291460 | tf_op jit(solution)/shard_map/while
  (92 other events, 789.8 us)
Sparse Core Ops, SparseCore 0:
  1055.5 195.2 all-gather.1
where the time goes:
time: 1590 us; the launch traced here: 1580 us
  local copies, waits for them, and re-layouts  427 us (27%)
  matrix products  403 us (25%)
  waiting for transfers between devices  388 us (24%)
  other arithmetic  219 us (14%)
  starting transfers between devices  124 us (8%)
  between operations  16.1 us (1%)
    unnamed x241, local copies, waits for them, and re-layouts  202 us
    sub x12, other arithmetic, _attend(): p = jax.nn.softmax(s, axis=-1).astype(jnp.bfloat16)  176 us
    all_gather x1, waiting for transfers between devices, body(): kvg = lax.all_gather(kv, 'cp', axis=1, tiled=True)  170 us
    dot_general x12, matrix products, _attend(): jnp.einsum('hgqk,khd->qhgd', p, v, preferred_element_type=jnp.float32)  139 us
    ppermute x20, waiting for transfers between devices, body(): blk_a = lax.ppermute(send_a, 'cp', fwd)  128 us
    dot_general x18, matrix products, _proj(): jnp.dot(n, w.reshape(n.shape[-1], -1), preferred_element_type=jnp.float32)  108 us
    dot_general x12, matrix products, _attend(): jnp.einsum('qhgd,khd->hgqk', q, k, preferred_element_type=jnp.float32)  92.1 us
    ppermute x20, waiting for transfers between devices, body(): blk_b = jnp.where(i == cp - 1, send_a, lax.ppermute(send_b, 'cp', bwd))  89.1 us
  transfers between devices with their start and end apart: 41, of which 29 were waited for; matrix products, arithmetic and copies ran while one was open for 26% of the time, Pallas kernels for 0%

commit v1 on v0

v1 whole, which is shorter than its diff:
```python
import functools
import math

import jax
import jax.numpy as jnp
from jax import lax
from jax.experimental import pallas as pl
from jax.experimental.pallas import tpu as pltpu
from jax.sharding import PartitionSpec as P

W = 1024
EPS = 1e-6
F32 = jnp.float32
BF16 = jnp.bfloat16
MESH = pl.DeviceIdType.MESH
CHUNKS = 8
SLOTS = 3
NEG = float('-inf')


def _dot(a, b):
    return jnp.dot(a, b, preferred_element_type=F32)


def _dot_nt(a, b):
    return lax.dot_general(a, b, (((1,), (1,)), ((), ())), preferred_element_type=F32)


def _for(n, body):
    lax.fori_loop(0, n, lambda j, c: (body(j), c)[1], 0)


def _barrier(cp, i, partner):
    sem = pltpu.get_barrier_semaphore()
    for nb in (lax.rem(i + 2, cp), lax.rem(i + cp - 2, cp), partner):
        pl.semaphore_signal(sem, inc=1, device_id={'cp': nb}, device_id_type=MESH)
    pl.semaphore_wait(sem, 3)


def _remote(src, dst, ssem, rsem, dev):
    return pltpu.make_async_remote_copy(src_ref=src, dst_ref=dst, send_sem=ssem, recv_sem=rsem,
                                        device_id={'cp': dev}, device_id_type=MESH)


def _norm(x, n, g):
    rows = 64 if x.shape[0] % 64 == 0 else x.shape[0]

    def blk(j):
        sl = pl.ds(pl.multiple_of(j * rows, rows), rows)
        v = x[sl, :]
        s = lax.rsqrt(jnp.mean(v * v, axis=-1, keepdims=True) + EPS)
        n[sl, :] = (v * s * g).astype(BF16)

    _for(x.shape[0] // rows, blk)


def _round_rows(x, dst):
    rows = 64 if x.shape[0] % 64 == 0 else x.shape[0]

    def blk(j):
        sl = pl.ds(pl.multiple_of(j * rows, rows), rows)
        v = x[sl, :].astype(BF16)
        if dst is None:
            x[sl, :] = v.astype(F32)
        else:
            dst[sl, :] = v

    _for(x.shape[0] // rows, blk)


def _load_rows(src, x):
    rows = 64 if x.shape[0] % 64 == 0 else x.shape[0]

    def blk(j):
        sl = pl.ds(pl.multiple_of(j * rows, rows), rows)
        x[sl, :] = src[sl, :].astype(F32)

    _for(x.shape[0] // rows, blk)


def _out_proj(x, o, wo, slot):
    d = x.shape[1]
    nb = min(512, d)

    def blk(j):
        sl = pl.ds(pl.multiple_of(j * nb, nb), nb)
        x[:, sl] += _dot(o[...], wo[slot, :, sl])

    _for(d // nb, blk)


def _local_kernel(cp, nloc, x_hbm, g_ref, wq_hbm, wk_hbm, wv_hbm, wo_hbm, xo_hbm, wkvo_hbm, wqo_hbm,
                  x, n, q, wkv, wq, wo, own, halo, stage, o, pq, pkv,
                  msem, ssem, wosem, send, extra, recv):
    t, d = x.shape
    r = t // 2
    hkv, dh = own.shape[0] // 2, own.shape[2] // 2
    nz = cp // 2
    i = lax.axis_index('cp')
    c = lax.rem(i, 2)
    z = lax.div(i, 2)
    partner = i + 1 - 2 * c
    last = z == nz - 1
    crows = stage.shape[1]
    nblk = crows // 256
    scale = dh ** -0.5 * math.log2(math.e)

    def yes():
        return z >= 0

    cc = (c, 1 - c)
    nxt_dev = (lax.rem(i + 2, cp), lax.rem(i + cp - 2, cp))
    nxt = (z + 1 < nz, z > 0)
    e2 = (z >= 1, yes())
    e4 = (z >= 2, yes())

    def hidx(par, s, p, h):
        return ((par * 2 + s) * 4 + p) * hkv + h

    def hs(par, s, p, h):
        return halo.at[hidx(par, s, p, h)]

    def copy(kind, s, h, par):
        ownr = own.at[s * hkv + h]
        sem = send.at[(kind * 2 + s) * hkv + h]
        if kind == 0:
            src, p, dev = ownr, 1, nxt_dev[s]
        elif kind == 1:
            src, p, dev = hs(par, s, 1, h), 3, nxt_dev[s]
        elif kind == 2:
            src, p, dev = ownr, 0, partner
        elif kind == 3:
            src, p, dev = hs(par, s, 1, h), 0, partner
        elif kind == 4:
            src, p, dev = hs(par, s, 1, h), 2, partner
        else:
            src, p, dev = hs(par, s, 3, h), 2, partner
        return _remote(src, hs(par, s, p, h), sem, recv.at[hidx(par, s, p, h)], dev)

    def cond(kind, s):
        lead, follow = cc[s] == 0, cc[s] == 1
        return (nxt[s], nxt[s] & e2[s], lead, follow & e2[s], lead & e2[s], follow & e4[s])[kind]

    def start(kind, s, h, par):
        pl.when(cond(kind, s))(lambda: copy(kind, s, h, par).start())

    def edge_copy(h, par):
        return _remote(own.at[h], hs(par, 1, 1, h), extra.at[h], recv.at[hidx(par, 1, 1, h)], partner)

    def edge_local(p, h, par):
        return pltpu.make_async_copy(hs(par, 0, p, h), hs(par, 1, 3, h), recv.at[hidx(par, 1, 3, h)])

    def arrived(s, p, h, par, when):
        slot = hs(par, s, p, h)
        pl.when(when)(lambda: pltpu.make_async_copy(slot, slot, recv.at[hidx(par, s, p, h)]).wait())

    def raw(kv, l, j):
        sl = pl.ds(pl.multiple_of(j * crows, 256), crows)
        slot = lax.rem(j, SLOTS)
        if kv:
            return (pltpu.make_async_copy(wk_hbm.at[l, sl], stage.at[slot, :, pl.ds(0, 128)], ssem.at[slot]),
                    pltpu.make_async_copy(wv_hbm.at[l, sl], stage.at[slot, :, pl.ds(128, 128)], ssem.at[SLOTS + slot]))
        return (pltpu.make_async_copy(wq_hbm.at[l, sl], stage.at[slot], ssem.at[slot]),)

    def prefetch(kv, l):
        for j in range(SLOTS):
            for cpy in raw(kv, l, j):
                cpy.start()

    def relayout(kv, l):
        unroll = 5 if nblk % 5 == 0 else 1

        def chunk(j):
            for cpy in raw(kv, l, j):
                cpy.wait()
            slot = lax.rem(j, SLOTS)

            def group(b):
                for u in range(unroll):
                    bb = b * unroll + u
                    blk = stage[slot, pl.ds(pl.multiple_of(bb * 256, 256), 256), :]
                    out = _dot(pkv[...] if kv else pq[...], blk).astype(BF16)
                    rows = pl.ds(pl.multiple_of((j * nblk + bb) * 32, 32), 32)
                    for a in range(8):
                        part = out[a * 32:(a + 1) * 32]
                        if kv:
                            h, lane = a // 2, (a % 2) * 128
                            wkv[h, rows, lane:lane + 128] = part[:, :128]
                            wkv[h, rows, dh + lane:dh + lane + 128] = part[:, 128:]
                        else:
                            wq[a // 2, rows, (a % 2) * dh:(a % 2 + 1) * dh] = part

            _for(nblk // unroll, group)

            @pl.when(j + SLOTS < CHUNKS)
            def _():
                for cpy in raw(kv, l, j + SLOTS):
                    cpy.start()

        _for(CHUNKS, chunk)

    def wo_copy(l, h):
        slot = lax.rem(h, 2)
        return pltpu.make_async_copy(wo_hbm.at[l, pl.ds(pl.multiple_of(h * 2 * dh, 2 * dh), 2 * dh)], wo.at[slot], wosem.at[slot])

    load_x = pltpu.make_async_copy(x_hbm, n, msem.at[0])
    load_x.start()
    prefetch(True, 0)
    wo_copy(0, 0).start()
    wo_copy(0, 1).start()

    @pl.when(z < 2)
    def _():
        def clear(j):
            par = lax.div(j, 4 * hkv)
            halo[par * 8 * hkv + lax.rem(j, 4 * hkv)] = jnp.zeros(halo.shape[1:], BF16)

        _for(8 * hkv, clear)

    _barrier(cp, i, partner)
    ro = lax.broadcasted_iota(jnp.int32, (256, 256), 0)
    co = lax.broadcasted_iota(jnp.int32, (256, 256), 1)
    pq[...] = jnp.where(co == (ro % 32) * 8 + ro // 32, 1.0, 0.0).astype(BF16)
    pkv[...] = jnp.where(co == (ro % 32) * 8 + ((ro // 32) % 2) * 4 + ro // 64, 1.0, 0.0).astype(BF16)
    relayout(True, 0)
    prefetch(False, 0)
    load_x.wait()
    _load_rows(n, x)
    _norm(x, n, g_ref[0])

    rows = lax.broadcasted_iota(jnp.int32, (2 * r, r), 0) % r
    cols = lax.broadcasted_iota(jnp.int32, (2 * r, r), 1)

    def attend(s, h, par):
        qv = q[s * hkv + h]
        ks = [own[s * hkv + h, :, :dh]] + [halo[hidx(par, s, p, h), :, :dh] for p in range(4)]
        vs = [own[s * hkv + h, :, dh:]] + [halo[hidx(par, s, p, h), :, dh:] for p in range(4)]
        sc = [_dot_nt(qv, k) for k in ks]
        sc[0] = jnp.where(cols <= rows, sc[0], NEG)
        sc[4] = jnp.where(cols > rows, sc[4], NEG)
        if s == 0:
            for b in range(1, 5):
                sc[b] = sc[b] + jnp.where(i >= b, 0.0, NEG).astype(F32)
        m = functools.reduce(jnp.maximum, sc).max(axis=1, keepdims=True)
        pr = [jnp.exp2((v - m) * scale) for v in sc]
        den = functools.reduce(jnp.add, pr).sum(axis=1, keepdims=True)
        num = functools.reduce(jnp.add, [_dot(a.astype(BF16), v) for a, v in zip(pr, vs)])
        out = (num / den).astype(BF16)
        o[s * r:(s + 1) * r, :dh] = out[:r]
        o[s * r:(s + 1) * r, dh:] = out[r:]

    def layer(l):
        par = lax.rem(l, 2)

        def kv_head(h):
            y = _dot(n[...], wkv[h]).astype(BF16)
            own[h] = y[:r]
            own[hkv + h] = y[r:]
            for s in range(2):
                start(0, s, h, par)
                start(2, s, h, par)
            pl.when(last)(lambda: edge_copy(h, par).start())

        _for(hkv, kv_head)

        @pl.when(l == 0)
        def _():
            relayout(False, 0)
        prefetch(True, l + 1)

        def q_group(h):
            y = _dot(n[...], wq[h]).astype(BF16)
            for s in range(2):
                q[s * hkv + h, :r] = y[s * r:(s + 1) * r, :dh]
                q[s * hkv + h, r:] = y[s * r:(s + 1) * r, dh:]

        _for(hkv, q_group)

        def forward(h):
            for s in range(2):
                arrived(s, 1, h, par, e2[s])
                for kind in (1, 3, 4):
                    start(kind, s, h, par)

        forward(0)
        relayout(True, l + 1)
        prefetch(False, l + 1)
        forward(1)
        relayout(False, l + 1)
        forward(2)
        forward(3)

        def head(h):
            arrived(0, 3, h, par, e4[0])
            start(5, 0, h, par)
            arrived(0, 0, h, par, (c == 1) | e2[0])
            arrived(0, 2, h, par, jnp.where(c == 1, z >= 1, z >= 2))
            pl.when(last & (c == 1))(lambda: edge_local(2, h, par).start())
            pl.when(last & (c == 0))(lambda: edge_local(0, h, par).start())
            arrived(1, 3, h, par, yes())
            start(5, 1, h, par)
            arrived(1, 0, h, par, yes())
            arrived(1, 2, h, par, yes())
            attend(0, h, par)
            attend(1, h, par)
            wo_copy(l, h).wait()
            _out_proj(x, o, wo, lax.rem(h, 2))

            @pl.when((h < hkv - 2) | (l < nloc - 1))
            def _():
                wrap = lax.div(h + 2, hkv)
                wo_copy(l + wrap, h + 2 - hkv * wrap).start()

        _for(hkv, head)

        def drain(h):
            for s in range(2):
                for kind in range(6):
                    pl.when(cond(kind, s))(lambda k=kind, s=s: copy(k, s, h, par).wait_send())
            pl.when(last)(lambda: edge_copy(h, par).wait_send())

        _for(hkv, drain)

        @pl.when(l < nloc - 1)
        def _():
            _round_rows(x, None)
            _norm(x, n, g_ref[l + 1])

    _for(nloc, layer)
    out_kv = pltpu.make_async_copy(wkv, wkvo_hbm, msem.at[1])
    out_q = pltpu.make_async_copy(wq, wqo_hbm, msem.at[2])
    out_kv.start()
    out_q.start()
    _round_rows(x, n)
    out_x = pltpu.make_async_copy(n, xo_hbm, msem.at[0])
    out_x.start()
    out_kv.wait()
    out_q.wait()
    out_x.wait()


def _global_kernel(cp, lay, x_hbm, g_ref, wkv_hbm, wq_hbm, wo_hbm, y_hbm,
                   x, q, kvg, acc, mx, den, wst, wo, o,
                   msem, wsem, wosem, isend, irecv, dsend, drecv):
    t, d = x.shape
    r = t // 2
    hkv, dh = q.shape[0] // 2, q.shape[2]
    nz = cp // 2
    i = lax.axis_index('cp')
    c = lax.rem(i, 2)
    z = lax.div(i, 2)
    partner = i + 1 - 2 * c
    scale = dh ** -0.5 * math.log2(math.e)
    nxt_dev = (lax.rem(i + 2, cp), lax.rem(i + cp - 2, cp))

    def run_of(s, k, core):
        if s == 0:
            return lax.rem(z - k + nz, nz) * 2 + core
        return 2 * cp - 1 - (z + k) * 2 - core

    def slot(s, k, core, h):
        return run_of(s, k, core) * hkv + h

    def has(s, k):
        return (k < nz) if s == 0 else (z + k < nz)

    def sends(s, k):
        return (k < nz - 1) if s == 0 else ((z + k < nz) & (z > 0))

    def sidx(s, k, h):
        return (s * nz + k) * hkv + h

    def ici(s, k, h):
        ref = kvg.at[slot(s, k, c, h)]
        return _remote(ref, ref, isend.at[sidx(s, k, h)], irecv.at[sidx(s, k + 1, h)], nxt_dev[s])

    def d2d(s, k, h):
        ref = kvg.at[slot(s, k, c, h)]
        return _remote(ref, ref, dsend.at[sidx(s, k, h)], drecv.at[sidx(s, k, h)], partner)

    def push(s, k, h):
        pl.when(sends(s, k))(lambda: ici(s, k, h).start())
        pl.when(has(s, k))(lambda: d2d(s, k, h).start())

    def got_ici(s, k, h):
        ref = kvg.at[slot(s, k, c, h)]
        pl.when(has(s, k))(lambda: pltpu.make_async_copy(ref, ref, irecv.at[sidx(s, k, h)]).wait())

    def got_d2d(s, k, h):
        ref = kvg.at[slot(s, k, 1 - c, h)]
        pl.when(has(s, k))(lambda: pltpu.make_async_copy(ref, ref, drecv.at[sidx(s, k, h)]).wait())

    def wtile(j):
        src = wkv_hbm.at[j] if j < hkv else wq_hbm.at[j - hkv]
        return pltpu.make_async_copy(src, wst.at[j % 2], wsem.at[j % 2])

    def wo_copy(h):
        sl = lax.rem(h, 2)
        return pltpu.make_async_copy(wo_hbm.at[lay, pl.ds(pl.multiple_of(h * 2 * dh, 2 * dh), 2 * dh)], wo.at[sl], wosem.at[sl])

    load_x = pltpu.make_async_copy(x_hbm, wo.at[0, :t], msem.at[0])
    load_x.start()
    wtile(0).start()
    wtile(1).start()
    _barrier(cp, i, partner)
    load_x.wait()
    n = wo.at[1, :t]
    _load_rows(wo.at[0, :t], x)
    _norm(x, n, g_ref[lay])
    for j in range(2 * hkv):
        wtile(j).wait()
        y = _dot(n[...], wst[j % 2]).astype(BF16)
        if j < hkv:
            kvg[slot(0, 0, c, j)] = y[:r]
            kvg[slot(1, 0, c, j)] = y[r:]
            for s in range(2):
                push(s, 0, j)
        else:
            for s in range(2):
                q[s * hkv + j - hkv, :r] = y[s * r:(s + 1) * r, :dh]
                q[s * hkv + j - hkv, r:] = y[s * r:(s + 1) * r, dh:]
        if j + 2 < 2 * hkv:
            wtile(j + 2).start()
    wo_copy(0).start()
    wo_copy(1).start()

    def init(j):
        acc[j] = jnp.zeros(acc.shape[1:], F32)
        mx[j] = jnp.full(mx.shape[1:], NEG, F32)
        den[j] = jnp.zeros(den.shape[1:], F32)

    _for(2 * hkv, init)
    rows = lax.broadcasted_iota(jnp.int32, (2 * r, r), 0) % r
    cols = lax.broadcasted_iota(jnp.int32, (2 * r, r), 1)

    def flash(qs, ks, k, h, masked):
        qi = qs * hkv + h
        qv = q[qi]
        sl = [slot(ks, k, core, h) for core in range(2)]
        sc = [_dot_nt(qv, kvg[a, :, :dh]) for a in sl]
        if masked:
            rq = run_of(qs, 0, c)
            sc = [jnp.where(cols - rows <= (rq - run_of(ks, k, core)) * r, v, NEG) for core, v in enumerate(sc)]
        old = mx[qi][:, :1]
        m = jnp.maximum(old, jnp.maximum(sc[0], sc[1]).max(axis=1, keepdims=True))
        a = jnp.exp2((old - m) * scale)
        pr = [jnp.exp2((v - m) * scale) for v in sc]
        dn = den[qi][:, :1] * a + (pr[0] + pr[1]).sum(axis=1, keepdims=True)
        acc[qi] = acc[qi] * a + (_dot(pr[0].astype(BF16), kvg[sl[0], :, dh:]) + _dot(pr[1].astype(BF16), kvg[sl[1], :, dh:]))
        mx[qi] = jnp.broadcast_to(m, mx.shape[1:])
        den[qi] = jnp.broadcast_to(dn, den.shape[1:])

    def step(k, h):
        for s in range(2):
            got_d2d(s, k, h)

        def job(j):
            qs = jnp.where(j < 2, 1, 0)
            run0 = jnp.where(j == 1, run_of(1, k, 0), run_of(0, k, 0))
            run1 = jnp.where(j == 1, run_of(1, k, 1), run_of(0, k, 1))
            ok = jnp.where(j == 1, z + k < nz, jnp.where(j == 2, z - k >= 0, z >= 0))
            pl.when(ok)(lambda: flash_at(qs * hkv + h, run0 * hkv + h, run1 * hkv + h))

        _for(3, job)

    def flash_at(qi, s0, s1):
        qv = q[qi]
        sc = [_dot_nt(qv, kvg[a, :, :dh]) for a in (s0, s1)]
        old = mx[qi][:, :1]
        m = jnp.maximum(old, jnp.maximum(sc[0], sc[1]).max(axis=1, keepdims=True))
        a = jnp.exp2((old - m) * scale)
        pr = [jnp.exp2((v - m) * scale) for v in sc]
        dn = den[qi][:, :1] * a + (pr[0] + pr[1]).sum(axis=1, keepdims=True)
        acc[qi] = acc[qi] * a + (_dot(pr[0].astype(BF16), kvg[s0, :, dh:]) + _dot(pr[1].astype(BF16), kvg[s1, :, dh:]))
        mx[qi] = jnp.broadcast_to(m, mx.shape[1:])
        den[qi] = jnp.broadcast_to(dn, den.shape[1:])

    def finish(h):
        for s in range(2):
            qi = s * hkv + h
            out = (acc[qi] / den[qi][:, :1]).astype(BF16)
            o[s * r:(s + 1) * r, :dh] = out[:r]
            o[s * r:(s + 1) * r, dh:] = out[r:]
        wo_copy(h).wait()
        _out_proj(x, o, wo, lax.rem(h, 2))
        pl.when(h + 2 < hkv)(lambda: wo_copy(h + 2).start())

    def main(j):
        k = 1 + lax.div(j, hkv)
        h = lax.rem(j, hkv)
        for s in range(2):
            got_ici(s, k, h)
            push(s, k, h)

        @pl.when(k == 1)
        def _():
            for s in range(2):
                got_d2d(s, 0, h)
            flash(0, 0, 0, h, True)
            flash(1, 0, 0, h, False)
            flash(1, 1, 0, h, True)

        jp = j - 1
        kp = 1 + lax.div(jp, hkv)
        hp = lax.rem(jp, hkv)

        @pl.when(j > 0)
        def _():
            step(kp, hp)
            pl.when(kp == nz - 1)(lambda: finish(hp))

    _for((nz - 1) * hkv, main)
    step(nz - 1, hkv - 1)
    finish(hkv - 1)
    _round_rows(x, wo.at[0, :t])
    out = pltpu.make_async_copy(wo.at[0, :t], y_hbm, msem.at[0])
    out.start()

    def drain(j):
        k = lax.div(j, hkv)
        h = lax.rem(j, hkv)
        for s in range(2):
            pl.when(sends(s, k))(lambda s=s: ici(s, k, h).wait_send())
            pl.when(has(s, k))(lambda s=s: d2d(s, k, h).wait_send())

    _for(nz * hkv, drain)
    out.wait()


def solution(mesh):
    cp = mesh.shape['cp']

    def body(x, g, wq, wk, wv, wo):
        t, d = x.shape
        r = t // 2
        nl = g.shape[0]
        hq, dh = wq.shape[2], wq.shape[3]
        hkv = wk.shape[2]
        assert (hq, hkv, dh, W) == (8, 4, 256, 4 * r)
        gf = g.astype(F32).reshape(nl, 1, d)
        wq2 = wq.reshape(nl, d * hq, dh)
        wk2, wv2 = (a.reshape(nl, d, hkv, 2, dh // 2).transpose(0, 1, 3, 2, 4).reshape(nl, d * hkv * 2, dh // 2) for a in (wk, wv))
        wo2 = wo.reshape(nl, hq * dh, d)
        hbm = pl.BlockSpec(memory_space=pl.ANY)
        vmem = pl.BlockSpec(memory_space=pltpu.VMEM)
        sems = pltpu.SemaphoreType.DMA
        shape = jax.ShapeDtypeStruct
        limit = 67043328
        tile = (hkv, d, 2 * dh)
        x1, wkv_l, wq_l = pl.pallas_call(
            functools.partial(_local_kernel, cp, nl - 1),
            out_shape=(shape((t, d), BF16), shape(tile, BF16), shape(tile, BF16)),
            in_specs=[hbm, vmem, hbm, hbm, hbm, hbm],
            out_specs=(hbm, hbm, hbm),
            scratch_shapes=[
                pltpu.VMEM((t, d), F32),
                pltpu.VMEM((t, d), BF16),
                pltpu.VMEM((2 * hkv, 2 * r, dh), BF16),
                pltpu.VMEM(tile, BF16),
                pltpu.VMEM(tile, BF16),
                pltpu.VMEM((2, 2 * dh, d), BF16),
                pltpu.VMEM((2 * hkv, r, 2 * dh), BF16),
                pltpu.VMEM((2 * 2 * 4 * hkv, r, 2 * dh), BF16),
                pltpu.VMEM((SLOTS, d * hq // CHUNKS, dh), BF16),
                pltpu.VMEM((t, 2 * dh), BF16),
                pltpu.VMEM((256, 256), BF16),
                pltpu.VMEM((256, 256), BF16),
                sems((3,)), sems((2 * SLOTS,)), sems((2,)), sems((6 * 2 * hkv,)), sems((hkv,)), sems((2 * 2 * 4 * hkv,)),
            ],
            compiler_params=pltpu.CompilerParams(collective_id=0, has_side_effects=True, vmem_limit_bytes=limit),
            name='local_layers',
        )(x, gf, wq2, wk2, wv2, wo2)
        nz = cp // 2
        return pl.pallas_call(
            functools.partial(_global_kernel, cp, nl - 1),
            out_shape=shape((t, d), BF16),
            in_specs=[hbm, vmem, hbm, hbm, hbm],
            out_specs=hbm,
            scratch_shapes=[
                pltpu.VMEM((t, d), F32),
                pltpu.VMEM((2 * hkv, 2 * r, dh), BF16),
                pltpu.VMEM((2 * cp * hkv, r, 2 * dh), BF16),
                pltpu.VMEM((2 * hkv, 2 * r, dh), F32),
                pltpu.VMEM((2 * hkv, 2 * r, 128), F32),
                pltpu.VMEM((2 * hkv, 2 * r, 128), F32),
                pltpu.VMEM((2, d, 2 * dh), BF16),
                pltpu.VMEM((2, 2 * dh, d), BF16),
                pltpu.VMEM((t, 2 * dh), BF16),
                sems((1,)), sems((2,)), sems((2,)),
                sems((2 * nz * hkv,)), sems((2 * nz * hkv,)), sems((2 * nz * hkv,)), sems((2 * nz * hkv,)),
            ],
            compiler_params=pltpu.CompilerParams(collective_id=1, has_side_effects=True, vmem_limit_bytes=limit),
            name='global_layer',
        )(x1, gf, wkv_l, wq_l, wo2)

    spec = P(('dp', 'cp'), None)
    return jax.shard_map(body, mesh=mesh, in_specs=(spec, P(), P(), P(), P(), P()), out_specs=spec, check_vma=False)
```

time: 1590 us -> 531 us (0.33)
  Pallas kernels: 0 us -> 526 us
  local copies, waits for them, and re-layouts: 427 us -> 4.84 us
  matrix products: 403 us -> 0 us
  waiting for transfers between devices: 388 us -> 0 us
  other arithmetic: 219 us -> 0 us
  starting transfers between devices: 124 us -> 0 us
  between operations: 16.1 us -> 0.02 us
    pallas_call x0 -> x2, Pallas kernels: none -> 526 us  [the longest x1 321 us: body(): pl.pallas_call(functools.partial(_local_kernel, cp, nl - 1), out_shape=(s...]
    dot_general x48 -> x0, matrix products: 403 us -> none  [the longest x12 139 us: _attend(): jnp.einsum('hgqk,khd->qhgd', p, v, preferred_element_type=jnp.float32)]
    ppermute x40 -> x0, waiting for transfers between devices: 217 us -> none  [the longest x20 128 us: body(): blk_a = lax.ppermute(send_a, 'cp', fwd)]
    unnamed x241 -> x1, local copies, waits for them, and re-layouts: 202 us -> 3.4 us
    sub x15 -> x0, other arithmetic: 176 us -> none  [the longest x12 176 us: _attend(): p = jax.nn.softmax(s, axis=-1).astype(jnp.bfloat16)]
    all_gather x1 -> x0, waiting for transfers between devices: 170 us -> none  [body(): kvg = lax.all_gather(kv, 'cp', axis=1, tiled=True)]
    slice x21 -> x0, local copies, waits for them, and re-layouts: 164 us -> none  [the longest x2 45.5 us: body(): kv = jnp.stack([_proj(n, wk[l]), _proj(n, wv[l])])]
    ppermute x40 -> x0, starting transfers between devices: 124 us -> none  [the longest x20 81.8 us: body(): blk_a = lax.ppermute(send_a, 'cp', fwd)]
  transfers between devices with their start and end apart: 41 -> 0, of which waited for: 29 -> 0; matrix products, arithmetic and copies ran while one was open for 26% -> 0% of each run, Pallas kernels for 0% -> 0%
where the time goes in v1:
time: 531 us
  Pallas kernels  526 us (99%)
    pallas_call x1, Pallas kernels, body(): pl.pallas_call(functools.partial(_local_kernel, cp, nl - 1), out_shape=(s...  321 us
    pallas_call x1, Pallas kernels, body(): pl.pallas_call(functools.partial(_global_kernel, cp, nl - 1), out_shape=s...  205 us

profile of v1, /device:TPU:21, one launch (start us, length us, event | category | flops | bytes accessed | tf_op | source)
XLA Modules:
  0.0 530.7 jit_solution(1076383612980372300)
XLA Ops:
  0.0 1.4 reshape.32.g_ref
  1.4 321.0 %local_layers.1 = (bf16[512,2560]{1,0:T(8,128)(2,1)}, bf16[4,2560,512]{2,1,0:T(8,128)(2,1)}, bf16[4,2560,512]{2,1,0:T(8,128)(2,1)}) custom-call(bf16[512,2560]{1,0:T(8,128)(2,1)} %x_hbm.1, f32[6,1,2560]{2,1,0:T(1,128)} %reshape.32.g_ref, bf16[6,20480,256]{2,1,0:T(8,128)(2,1)} %bitcast.14, bf16[6,20480,128]{2,1,0:T(8,128)(2,1)} %bitcast.15, ...), custom_call_target="tpu_custom_call" | custom-call | tf_op jit(solution)/shard_map/local_layers/pallas_call | solution.py:550
  322.5 204.8 %global_layer.1 = bf16[512,2560]{1,0:T(8,128)(2,1)} custom-call(bf16[512,2560]{1,0:T(8,128)(2,1)} %get-tuple-element.8.x_hbm, f32[6,1,2560]{2,1,0:T(1,128)} %reshape.32.g_ref, bf16[4,2560,512]{2,1,0:T(8,128)(2,1)} %get-tuple-element.9.wkv_hbm, bf16[4,2560,512]{2,1,0:T(8,128)(2,1)} %get-tuple-element.10.wq_hbm, bf16[6,2048,2560]{2,1,0:T(8,128)(2,1)} %bitcast.13), custom_call_target="tpu_custom_call" | custom-call | tf_op jit(solution)/shard_map/global_layer/pallas_call | solution.py:574
  527.3 3.4 copy.10

commit v2 on v1

v2 whole, which is shorter than its diff:
```python
import functools
import math

import jax
import jax.numpy as jnp
from jax import lax
from jax.experimental import pallas as pl
from jax.experimental.pallas import tpu as pltpu
from jax.sharding import PartitionSpec as P

W = 1024
EPS = 1e-6
F32 = jnp.float32
BF16 = jnp.bfloat16
MESH = pl.DeviceIdType.MESH
CHUNKS = 16
SLOTS = 6
NEG = float('-inf')


def _dot(a, b):
    return jnp.dot(a, b, preferred_element_type=F32)


def _dot_nt(a, b):
    return lax.dot_general(a, b, (((1,), (1,)), ((), ())), preferred_element_type=F32)


def _for(n, body):
    lax.fori_loop(0, n, lambda j, c: (body(j), c)[1], 0)


def _barrier(cp, i, partner):
    sem = pltpu.get_barrier_semaphore()
    for nb in (lax.rem(i + 2, cp), lax.rem(i + cp - 2, cp), partner):
        pl.semaphore_signal(sem, inc=1, device_id={'cp': nb}, device_id_type=MESH)
    pl.semaphore_wait(sem, 3)


def _remote(src, dst, ssem, rsem, dev):
    return pltpu.make_async_remote_copy(src_ref=src, dst_ref=dst, send_sem=ssem, recv_sem=rsem,
                                        device_id={'cp': dev}, device_id_type=MESH)


def _blocks(lo, n, body):
    rows = 64

    def blk(j):
        body(pl.ds(pl.multiple_of(lo + j * rows, rows), rows))

    _for(n // rows, blk)


def _norm(x, n, g, lo, cnt):
    def blk(sl):
        v = x[sl, :].astype(BF16).astype(F32)
        x[sl, :] = v
        s = lax.rsqrt(jnp.mean(v * v, axis=-1, keepdims=True) + EPS)
        n[sl, :] = (v * s * g).astype(BF16)

    _blocks(lo, cnt, blk)


def _cast_rows(src, dst):
    def blk(sl):
        dst[sl, :] = src[sl, :].astype(dst.dtype)

    _blocks(0, src.shape[0], blk)


def _turn(eye, a):
    return _dot_nt(eye[...], a).astype(BF16)


def _scores(k, qt):
    return _dot(k.reshape(-1, k.shape[-1]), qt)


def _eye():
    ro = lax.broadcasted_iota(jnp.int32, (256, 256), 0)
    co = lax.broadcasted_iota(jnp.int32, (256, 256), 1)
    return jnp.where(ro == co, 1.0, 0.0).astype(BF16)


def _out_proj(x, lo, o, wo, slot, rows):
    d = x.shape[1]
    nb = min(512, d)
    for j in range(d // nb):
        sl = slice(j * nb, (j + 1) * nb)
        x[lo:lo + rows, sl] += _dot(o[lo:lo + rows, :], wo[slot, :, sl])


def _store_o(eye, o, s, r, ot):
    dh = ot.shape[0]
    ob = ot.astype(BF16)
    for g in range(2):
        o[s * r:(s + 1) * r, g * dh:(g + 1) * dh] = _turn(eye, ob[:, g * r:(g + 1) * r])


def _local_kernel(cp, nloc, x_hbm, g_ref, wq_hbm, wk_hbm, wv_hbm, wo_hbm, xo_hbm, wkvo_hbm, wqo_hbm,
                  x, n, q, wkv, wq, wo, own, near, far, stage, o, pq, pkv,
                  msem, ssem, wosem, send, extra, recv):
    t, d = x.shape
    r = t // 2
    hkv, dh = own.shape[0] // 2, own.shape[2] // 2
    nz = cp // 2
    i = lax.axis_index('cp')
    c = lax.rem(i, 2)
    z = lax.div(i, 2)
    partner = i + 1 - 2 * c
    last = z == nz - 1
    crows = stage.shape[1]
    nblk = crows // 256
    scale = dh ** -0.5 * math.log2(math.e)

    def yes():
        return z >= 0

    cc = (c, 1 - c)
    nxt_dev = (lax.rem(i + 2, cp), lax.rem(i + cp - 2, cp))
    nxt = (z + 1 < nz, z > 0)
    e2 = (z >= 1, yes())
    e4 = (z >= 2, yes())

    def hs(par, s, p, h):
        if p < 2:
            return near.at[((par * 2 + s) * hkv + h) * 2 + p]
        return far.at[(s * hkv + h) * 2 + p - 2]

    def rsem(par, s, p, h):
        return recv.at[((par * 2 + s) * 4 + p) * hkv + h]

    def copy(kind, s, h, par):
        ownr = own.at[s * hkv + h]
        sem = send.at[(kind * 2 + s) * hkv + h]
        if kind == 0:
            src, p, dev = ownr, 1, nxt_dev[s]
        elif kind == 1:
            src, p, dev = hs(par, s, 1, h), 3, nxt_dev[s]
        elif kind == 2:
            src, p, dev = ownr, 0, partner
        elif kind == 3:
            src, p, dev = hs(par, s, 1, h), 0, partner
        elif kind == 4:
            src, p, dev = hs(par, s, 1, h), 2, partner
        else:
            src, p, dev = hs(par, s, 3, h), 2, partner
        return _remote(src, hs(par, s, p, h), sem, rsem(par, s, p, h), dev)

    def cond(kind, s):
        lead, follow = cc[s] == 0, cc[s] == 1
        return (nxt[s], nxt[s] & e2[s], lead, follow & e2[s], lead & e2[s], follow & e4[s])[kind]

    def start(kind, s, h, par):
        pl.when(cond(kind, s))(lambda: copy(kind, s, h, par).start())

    def edge_copy(h, par):
        return _remote(own.at[h], hs(par, 1, 1, h), extra.at[h], rsem(par, 1, 1, h), partner)

    def edge_local(p, h, par):
        return pltpu.make_async_copy(hs(par, 0, p, h), hs(par, 1, 3, h), rsem(par, 1, 3, h))

    def arrived(s, p, h, par, when):
        slot = hs(par, s, p, h)
        pl.when(when)(lambda: pltpu.make_async_copy(slot, slot, rsem(par, s, p, h)).wait())

    def raw(kv, l, j):
        sl = pl.ds(pl.multiple_of(j * crows, 256), crows)
        slot = lax.rem(j, SLOTS)
        if kv:
            return (pltpu.make_async_copy(wk_hbm.at[l, sl], stage.at[slot, :, pl.ds(0, 128)], ssem.at[slot]),
                    pltpu.make_async_copy(wv_hbm.at[l, sl], stage.at[slot, :, pl.ds(128, 128)], ssem.at[SLOTS + slot]))
        return (pltpu.make_async_copy(wq_hbm.at[l, sl], stage.at[slot], ssem.at[slot]),)

    def prefetch(kv, l):
        for j in range(SLOTS):
            for cpy in raw(kv, l, j):
                cpy.start()

    def relayout(kv, l):
        def chunk(j):
            for cpy in raw(kv, l, j):
                cpy.wait()
            slot = lax.rem(j, SLOTS)
            for b in range(nblk):
                blk = stage[slot, b * 256:(b + 1) * 256, :]
                out = _dot(pkv[...] if kv else pq[...], blk).astype(BF16)
                rows = pl.ds(pl.multiple_of((j * nblk + b) * 32, 32), 32)
                for a in range(8):
                    part = out[a * 32:(a + 1) * 32]
                    if kv:
                        h, lane = a // 2, (a % 2) * 128
                        wkv[h, rows, lane:lane + 128] = part[:, :128]
                        wkv[h, rows, dh + lane:dh + lane + 128] = part[:, 128:]
                    else:
                        wq[a // 2, rows, (a % 2) * dh:(a % 2 + 1) * dh] = part

            @pl.when(j + SLOTS < CHUNKS)
            def _():
                for cpy in raw(kv, l, j + SLOTS):
                    cpy.start()

        _for(CHUNKS, chunk)

    def wo_copy(l, h):
        slot = lax.rem(h, 2)
        return pltpu.make_async_copy(wo_hbm.at[l, pl.ds(pl.multiple_of(h * 2 * dh, 2 * dh), 2 * dh)], wo.at[slot], wosem.at[slot])

    load_x = pltpu.make_async_copy(x_hbm, n, msem.at[0])
    prefetch(True, 0)
    load_x.start()

    @pl.when(z < 2)
    def _():
        def clear(j):
            near[lax.div(j, 2 * hkv) * 4 * hkv + lax.rem(j, 2 * hkv)] = jnp.zeros(near.shape[1:], BF16)

        def clear_far(j):
            far[j] = jnp.zeros(far.shape[1:], BF16)

        _for(4 * hkv, clear)
        _for(2 * hkv, clear_far)

    _barrier(cp, i, partner)
    ro = lax.broadcasted_iota(jnp.int32, (256, 256), 0)
    co = lax.broadcasted_iota(jnp.int32, (256, 256), 1)
    pq[...] = jnp.where(co == (ro % 32) * 8 + ro // 32, 1.0, 0.0).astype(BF16)
    pkv[...] = jnp.where(co == (ro % 32) * 8 + ((ro // 32) % 2) * 4 + ro // 64, 1.0, 0.0).astype(BF16)
    rows = lax.broadcasted_iota(jnp.int32, (2 * r, r), 0) % r
    cols = lax.broadcasted_iota(jnp.int32, (2 * r, r), 1)

    def attend(s, h, par):
        qi = s * hkv + h
        qv = q[qi]
        jn = ((par * 2 + s) * hkv + h) * 2
        jf = qi * 2
        sn = _dot_nt(qv, near[pl.ds(jn, 2), :, :dh].reshape(2 * r, dh))
        sf = _dot_nt(qv, far[pl.ds(jf, 2), :, :dh].reshape(2 * r, dh))
        sc = [jnp.where(cols <= rows, _dot_nt(qv, own[qi, :, :dh]), NEG), sn[:, :r], sn[:, r:],
              sf[:, :r], jnp.where(cols > rows, sf[:, r:], NEG)]
        if s == 0:
            for b in range(1, 5):
                sc[b] = sc[b] + jnp.where(i >= b, 0.0, NEG).astype(F32)
        m = functools.reduce(jnp.maximum, sc).max(axis=1, keepdims=True)
        pr = [jnp.exp2((v - m) * scale) for v in sc]
        den = functools.reduce(jnp.add, pr).sum(axis=1, keepdims=True)
        vs = [own[qi, :, dh:], near[jn, :, dh:], near[jn + 1, :, dh:], far[jf, :, dh:], far[jf + 1, :, dh:]]
        num = functools.reduce(jnp.add, [_dot(a.astype(BF16), v) for a, v in zip(pr, vs)])
        out = (num / den).astype(BF16)
        o[s * r:(s + 1) * r, :dh] = out[:r]
        o[s * r:(s + 1) * r, dh:] = out[r:]

    def kv_store(s, h, y):
        own[s * hkv + h] = y

    def kv_send(s, h, par):
        start(0, s, h, par)
        start(2, s, h, par)
        if s == 0:
            pl.when(last)(lambda: edge_copy(h, par).start())

    def kv_first(s, par):
        kv_store(s, 0, _dot(n[s * r:(s + 1) * r, :], wkv[0]).astype(BF16))
        kv_send(s, 0, par)

    def drain(s, h, par):
        for kind in range(6):
            pl.when(cond(kind, s))(lambda k=kind: copy(k, s, h, par).wait_send())
        if s == 0:
            pl.when(last)(lambda: edge_copy(h, par).wait_send())

    relayout(True, 0)
    load_x.wait()
    prefetch(False, 0)
    _cast_rows(n, x)
    for s in range(2):
        _norm(x, n, g_ref[0], s * r, r)
        kv_first(s, 0)
    wo_copy(0, 0).start()
    wo_copy(0, 1).start()

    def layer(l):
        par = lax.rem(l, 2)

        def kv_head(j):
            h = j + 1
            y = _dot(n[...], wkv[h]).astype(BF16)
            for s in range(2):
                kv_store(s, h, y[s * r:(s + 1) * r])
                kv_send(s, h, par)

        _for(hkv - 1, kv_head)

        @pl.when(l == 0)
        def _():
            relayout(False, 0)
        prefetch(True, l + 1)

        def q_group(h):
            y = _dot(n[...], wq[h]).astype(BF16)
            for s in range(2):
                q[s * hkv + h, :r] = y[s * r:(s + 1) * r, :dh]
                q[s * hkv + h, r:] = y[s * r:(s + 1) * r, dh:]

        _for(hkv, q_group)

        def forward(h):
            for s in range(2):
                arrived(s, 1, h, par, e2[s])
                arrived(s, 0, h, par, cc[s] == 1)
            for s in range(2):
                for kind in (1, 3, 4):
                    start(kind, s, h, par)

        forward(0)
        relayout(True, l + 1)
        prefetch(False, l + 1)
        forward(1)
        relayout(False, l + 1)
        forward(2)
        forward(3)

        def far_ready(s, h):
            arrived(s, 0, h, par, (cc[s] == 0) & e2[s])
            arrived(s, 3, h, par, e4[s])
            start(5, s, h, par)

        def far_wait(s, h):
            arrived(s, 2, h, par, jnp.where(cc[0] == 1, z >= 1, z >= 2) if s == 0 else yes())
            if s == 0:
                pl.when(last & (c == 1))(lambda: edge_local(2, h, par).start())
                pl.when(last & (c == 0))(lambda: edge_local(0, h, par).start())

        def next_wo(h):
            @pl.when((h < hkv - 2) | (l < nloc - 1))
            def _():
                wrap = lax.div(h + 2, hkv)
                wo_copy(l + wrap, h + 2 - hkv * wrap).start()

        def head(h):
            far_ready(0, h)
            far_wait(0, h)
            far_ready(1, h)
            far_wait(1, h)
            attend(0, h, par)
            attend(1, h, par)
            wo_copy(l, h).wait()
            _out_proj(x, 0, o, wo, lax.rem(h, 2), t)
            next_wo(h)

        _for(hkv - 1, head)
        h3 = hkv - 1
        wo_copy(l, h3).wait()

        def tail(s):
            far_ready(s, h3)
            far_wait(s, h3)
            attend(s, h3, par)
            _out_proj(x, s * r, o, wo, h3 % 2, r)
            if s == 0:
                _for(hkv - 1, lambda h: (drain(0, h, par), drain(1, h, par)))
            drain(s, h3, par)

            @pl.when(l < nloc - 1)
            def _():
                _norm(x, n, g_ref[l + 1], s * r, r)
                kv_first(s, 1 - par)

        tail(0)
        tail(1)
        next_wo(h3)

    _for(nloc, layer)
    out_kv = pltpu.make_async_copy(wkv, wkvo_hbm, msem.at[1])
    out_q = pltpu.make_async_copy(wq, wqo_hbm, msem.at[2])
    out_kv.start()
    out_q.start()
    _cast_rows(x, n)
    out_x = pltpu.make_async_copy(n, xo_hbm, msem.at[0])
    out_x.start()
    out_kv.wait()
    out_q.wait()
    out_x.wait()


def _global_kernel(cp, lay, x_hbm, g_ref, wkv_hbm, wq_hbm, wo_hbm, y_hbm,
                   x, qt, kvg, acc, ml, wst, wo, o, eye,
                   msem, wsem, wosem, isend, irecv, dsend, drecv):
    t, d = x.shape
    r = t // 2
    hkv, dh = qt.shape[0] // 2, qt.shape[1]
    nz = cp // 2
    i = lax.axis_index('cp')
    c = lax.rem(i, 2)
    z = lax.div(i, 2)
    partner = i + 1 - 2 * c
    scale = dh ** -0.5 * math.log2(math.e)
    nxt_dev = (lax.rem(i + 2, cp), lax.rem(i + cp - 2, cp))

    def pair_of(s, k):
        return lax.rem(z - k + nz, nz) if s == 0 else cp - 1 - (z + k)

    def in_pair(s, core):
        return core if s == 0 else 1 - core

    def slot(s, k, core, h):
        return (pair_of(s, k) * hkv + h) * 2 + in_pair(s, core)

    def has(s, k):
        return (k < nz) if s == 0 else (z + k < nz)

    def sends(s, k):
        return (k < nz - 1) if s == 0 else ((z + k < nz) & (z > 0))

    def sidx(s, k, h):
        return (s * nz + k) * hkv + h

    def ici(s, k, h):
        ref = kvg.at[slot(s, k, c, h)]
        return _remote(ref, ref, isend.at[sidx(s, k, h)], irecv.at[sidx(s, k + 1, h)], nxt_dev[s])

    def d2d(s, k, h):
        ref = kvg.at[slot(s, k, c, h)]
        return _remote(ref, ref, dsend.at[sidx(s, k, h)], drecv.at[sidx(s, k, h)], partner)

    def push(s, k, h):
        pl.when(sends(s, k))(lambda: ici(s, k, h).start())
        pl.when(has(s, k))(lambda: d2d(s, k, h).start())

    def got_ici(s, k, h):
        ref = kvg.at[slot(s, k, c, h)]
        pl.when(has(s, k))(lambda: pltpu.make_async_copy(ref, ref, irecv.at[sidx(s, k, h)]).wait())

    def got_d2d(s, k, h):
        ref = kvg.at[slot(s, k, 1 - c, h)]
        pl.when(has(s, k))(lambda: pltpu.make_async_copy(ref, ref, drecv.at[sidx(s, k, h)]).wait())

    def wtile(j):
        src = wkv_hbm.at[j] if j < hkv else wq_hbm.at[j - hkv]
        return pltpu.make_async_copy(src, wst.at[j % 2], wsem.at[j % 2])

    def wo_copy(h):
        sl = lax.rem(h, 2)
        return pltpu.make_async_copy(wo_hbm.at[lay, pl.ds(pl.multiple_of(h * 2 * dh, 2 * dh), 2 * dh)], wo.at[sl], wosem.at[sl])

    load_x = pltpu.make_async_copy(x_hbm, wo.at[0, :t], msem.at[0])
    load_x.start()
    wtile(0).start()
    wtile(1).start()
    eye[...] = _eye()
    _barrier(cp, i, partner)
    load_x.wait()
    n = wo.at[1, :t]
    _cast_rows(wo.at[0, :t], x)
    _norm(x, n, g_ref[lay], 0, t)
    for j in range(2 * hkv):
        wtile(j).wait()
        y = _dot(n[...], wst[j % 2]).astype(BF16)
        for s in range(2):
            ys = y[s * r:(s + 1) * r]
            if j < hkv:
                own = slot(s, 0, c, j)
                kvg[own, :, :dh] = ys[:, :dh]
                kvg[own, :, dh:] = _turn(eye, ys[:, dh:])
                push(s, 0, j)
            else:
                for g in range(2):
                    qt[s * hkv + j - hkv, :, g * r:(g + 1) * r] = _turn(eye, ys[:, g * dh:(g + 1) * dh])
        if j + 2 < 2 * hkv:
            wtile(j + 2).start()
    wo_copy(0).start()
    wo_copy(1).start()

    def init(j):
        acc[j] = jnp.zeros(acc.shape[1:], F32)
        ml[j, 0:1, :] = jnp.full((1, 2 * r), NEG, F32)
        ml[j, 1:2, :] = jnp.zeros((1, 2 * r), F32)

    _for(2 * hkv, init)
    keys = lax.broadcasted_iota(jnp.int32, (2 * r, 2 * r), 0)
    toks = lax.broadcasted_iota(jnp.int32, (2 * r, 2 * r), 1) % r

    def flash(qi, pair, h, off=None):
        j = (pair * hkv + h) * 2
        sc = _scores(kvg[pl.ds(j, 2), :, :dh], qt[qi])
        if off is not None:
            sc = jnp.where(keys - toks <= off, sc, NEG)
        old = ml[qi, 0:1, :]
        m = jnp.maximum(old, sc.max(axis=0, keepdims=True))
        a = jnp.exp2((old - m) * scale)
        pr = jnp.exp2((sc - m) * scale)
        ml[qi, 0:1, :] = m
        ml[qi, 1:2, :] = ml[qi, 1:2, :] * a + pr.sum(axis=0, keepdims=True)
        pb = pr.astype(BF16)
        acc[qi] = acc[qi] * a + (_dot(kvg[j, :, dh:], pb[:r]) + _dot(kvg[j + 1, :, dh:], pb[r:]))

    def step(k, h):
        for s in range(2):
            got_d2d(s, k, h)

        def job(j):
            qs = jnp.where(j < 2, 1, 0)
            pair = jnp.where(j == 1, pair_of(1, k), pair_of(0, k))
            ok = jnp.where(j == 1, z + k < nz, jnp.where(j == 2, z - k >= 0, z >= 0))
            pl.when(ok)(lambda: flash(qs * hkv + h, pair, h))

        _for(3, job)

    def finish(h):
        for s in range(2):
            qi = s * hkv + h
            _store_o(eye, o, s, r, acc[qi] * (1.0 / ml[qi, 1:2, :]))
        wo_copy(h).wait()
        _out_proj(x, 0, o, wo, lax.rem(h, 2), t)
        pl.when(h + 2 < hkv)(lambda: wo_copy(h + 2).start())

    def main(j):
        k = 1 + lax.div(j, hkv)
        h = lax.rem(j, hkv)
        for s in range(2):
            got_ici(s, k, h)
            push(s, k, h)

        @pl.when(k == 1)
        def _():
            for s in range(2):
                got_d2d(s, 0, h)
            flash(h, pair_of(0, 0), h, c * r)
            flash(hkv + h, pair_of(0, 0), h)
            flash(hkv + h, pair_of(1, 0), h, (1 - c) * r)

        jp = j - 1
        kp = 1 + lax.div(jp, hkv)
        hp = lax.rem(jp, hkv)

        @pl.when(j > 0)
        def _():
            step(kp, hp)
            pl.when(kp == nz - 1)(lambda: finish(hp))

    _for((nz - 1) * hkv, main)
    step(nz - 1, hkv - 1)
    finish(hkv - 1)
    _cast_rows(x, wo.at[0, :t])
    out = pltpu.make_async_copy(wo.at[0, :t], y_hbm, msem.at[0])
    out.start()

    def drain(j):
        k = lax.div(j, hkv)
        h = lax.rem(j, hkv)
        for s in range(2):
            pl.when(sends(s, k))(lambda s=s: ici(s, k, h).wait_send())
            pl.when(has(s, k))(lambda s=s: d2d(s, k, h).wait_send())

    _for(nz * hkv, drain)
    out.wait()


def solution(mesh):
    cp = mesh.shape['cp']

    def body(x, g, wq, wk, wv, wo):
        t, d = x.shape
        r = t // 2
        nl = g.shape[0]
        hq, dh = wq.shape[2], wq.shape[3]
        hkv = wk.shape[2]
        assert (hq, hkv, dh, r, W) == (8, 4, 256, 256, 1024)
        gf = g.astype(F32).reshape(nl, 1, d)
        wq2 = wq.reshape(nl, d * hq, dh)
        wk2, wv2 = (a.reshape(nl, d, hkv, 2, dh // 2).transpose(0, 1, 3, 2, 4).reshape(nl, d * hkv * 2, dh // 2) for a in (wk, wv))
        wo2 = wo.reshape(nl, hq * dh, d)
        hbm = pl.BlockSpec(memory_space=pl.ANY)
        vmem = pl.BlockSpec(memory_space=pltpu.VMEM)
        sems = pltpu.SemaphoreType.DMA
        shape = jax.ShapeDtypeStruct
        limit = 67043328
        tile = (hkv, d, 2 * dh)
        x1, wkv_l, wq_l = pl.pallas_call(
            functools.partial(_local_kernel, cp, nl - 1),
            out_shape=(shape((t, d), BF16), shape(tile, BF16), shape(tile, BF16)),
            in_specs=[hbm, vmem, hbm, hbm, hbm, hbm],
            out_specs=(hbm, hbm, hbm),
            scratch_shapes=[
                pltpu.VMEM((t, d), F32),
                pltpu.VMEM((t, d), BF16),
                pltpu.VMEM((2 * hkv, 2 * r, dh), BF16),
                pltpu.VMEM(tile, BF16),
                pltpu.VMEM(tile, BF16),
                pltpu.VMEM((2, 2 * dh, d), BF16),
                pltpu.VMEM((2 * hkv, r, 2 * dh), BF16),
                pltpu.VMEM((2 * 2 * hkv * 2, r, 2 * dh), BF16),
                pltpu.VMEM((2 * hkv * 2, r, 2 * dh), BF16),
                pltpu.VMEM((SLOTS, d * hq // CHUNKS, dh), BF16),
                pltpu.VMEM((t, 2 * dh), BF16),
                pltpu.VMEM((256, 256), BF16),
                pltpu.VMEM((256, 256), BF16),
                sems((3,)), sems((2 * SLOTS,)), sems((2,)), sems((6 * 2 * hkv,)), sems((hkv,)), sems((2 * 2 * 4 * hkv,)),
            ],
            compiler_params=pltpu.CompilerParams(collective_id=0, has_side_effects=True, vmem_limit_bytes=limit),
            name='local_layers',
        )(x, gf, wq2, wk2, wv2, wo2)
        nz = cp // 2
        return pl.pallas_call(
            functools.partial(_global_kernel, cp, nl - 1),
            out_shape=shape((t, d), BF16),
            in_specs=[hbm, vmem, hbm, hbm, hbm],
            out_specs=hbm,
            scratch_shapes=[
                pltpu.VMEM((t, d), F32),
                pltpu.VMEM((2 * hkv, dh, 2 * r), BF16),
                pltpu.VMEM((2 * cp * hkv, r, 2 * dh), BF16),
                pltpu.VMEM((2 * hkv, dh, 2 * r), F32),
                pltpu.VMEM((2 * hkv, 8, 2 * r), F32),
                pltpu.VMEM((2, d, 2 * dh), BF16),
                pltpu.VMEM((2, 2 * dh, d), BF16),
                pltpu.VMEM((t, 2 * dh), BF16),
                pltpu.VMEM((256, 256), BF16),
                sems((1,)), sems((2,)), sems((2,)),
                sems((2 * nz * hkv,)), sems((2 * nz * hkv,)), sems((2 * nz * hkv,)), sems((2 * nz * hkv,)),
            ],
            compiler_params=pltpu.CompilerParams(collective_id=1, has_side_effects=True, vmem_limit_bytes=limit),
            name='global_layer',
        )(x1, gf, wkv_l, wq_l, wo2)

    spec = P(('dp', 'cp'), None)
    return jax.shard_map(body, mesh=mesh, in_specs=(spec, P(), P(), P(), P(), P()), out_specs=spec, check_vma=False)
```

time: 531 us -> 505 us (0.951)
  Pallas kernels: 526 us -> 500 us
    pallas_call x1, Pallas kernels: 205 us -> 186 us  [body(): pl.pallas_call(functools.partial(_global_kernel, cp, nl - 1), out_shape=s...]
    pallas_call x1, Pallas kernels: 321 us -> 314 us  [body(): pl.pallas_call(functools.partial(_local_kernel, cp, nl - 1), out_shape=(s...]
where the time goes in v2:
time: 505 us
  Pallas kernels  500 us (99%)
    pallas_call x1, Pallas kernels, body(): pl.pallas_call(functools.partial(_local_kernel, cp, nl - 1), out_shape=(s...  314 us
    pallas_call x1, Pallas kernels, body(): pl.pallas_call(functools.partial(_global_kernel, cp, nl - 1), out_shape=s...  186 us

profile of v2, /device:TPU:21, one launch (start us, length us, event | category | flops | bytes accessed | tf_op | source)
XLA Modules:
  0.0 504.8 jit_solution(11581549259775533605)
XLA Ops:
  0.0 1.4 reshape.32.g_ref
  1.4 314.1 %local_layers.1 = (bf16[512,2560]{1,0:T(8,128)(2,1)}, bf16[4,2560,512]{2,1,0:T(8,128)(2,1)}, bf16[4,2560,512]{2,1,0:T(8,128)(2,1)}) custom-call(bf16[512,2560]{1,0:T(8,128)(2,1)} %x_hbm.1, f32[6,1,2560]{2,1,0:T(1,128)} %reshape.32.g_ref, bf16[6,20480,256]{2,1,0:T(8,128)(2,1)} %bitcast.14, bf16[6,20480,128]{2,1,0:T(8,128)(2,1)} %bitcast.15, ...), custom_call_target="tpu_custom_call" | custom-call | tf_op jit(solution)/shard_map/local_layers/pallas_call | solution.py:579
  315.6 185.8 %global_layer.1 = bf16[512,2560]{1,0:T(8,128)(2,1)} custom-call(bf16[512,2560]{1,0:T(8,128)(2,1)} %get-tuple-element.8.x_hbm, f32[6,1,2560]{2,1,0:T(1,128)} %reshape.32.g_ref, bf16[4,2560,512]{2,1,0:T(8,128)(2,1)} %get-tuple-element.9.wkv_hbm, bf16[4,2560,512]{2,1,0:T(8,128)(2,1)} %get-tuple-element.10.wq_hbm, bf16[6,2048,2560]{2,1,0:T(8,128)(2,1)} %bitcast.13), custom_call_target="tpu_custom_call" | custom-call | tf_op jit(solution)/shard_map/global_layer/pallas_call | solution.py:604
  501.4 3.4 copy.10

commit v3 on v0

v3 whole, which is shorter than its diff:
```python
import functools
import math

import jax
import jax.numpy as jnp
from jax import lax
from jax.experimental import pallas as pl
from jax.experimental.pallas import tpu as pltpu
from jax.sharding import PartitionSpec as P

W = 1024
EPS = 1e-6
F32 = jnp.float32
BF16 = jnp.bfloat16
MESH = pl.DeviceIdType.MESH
STAGES = 4
NEG = float('-inf')

NEAR, FAR, OWN, WKV = 0, 32, 48, 56


def _dot(a, b):
    return jnp.dot(a, b, preferred_element_type=F32)


def _dot_nt(a, b):
    return lax.dot_general(a, b, (((1,), (1,)), ((), ())), preferred_element_type=F32)


def _for(n, body):
    lax.fori_loop(0, n, lambda j, c: (body(j), c)[1], 0)


def _pick(j, *vals):
    out = vals[-1]
    for k in range(len(vals) - 2, -1, -1):
        out = jnp.where(j == k, vals[k], out)
    return out


def _remote(src, dst, ssem, rsem, dev):
    return pltpu.make_async_remote_copy(src_ref=src, dst_ref=dst, send_sem=ssem, recv_sem=rsem,
                                        device_id={'cp': dev}, device_id_type=MESH)


def _blocks(lo, n, body):
    rows = 64

    def blk(j):
        body(pl.ds(pl.multiple_of(lo + j * rows, rows), rows))

    _for(n // rows, blk)


def _kernel(cp, x_hbm, g_ref, wq_hbm, wk_hbm, wv_hbm, wo_hbm, y_hbm,
            x, n, q, pool, wo, stage, o, acc, ml, gs, pq, pkv, eye,
            msem, ssem, wosem, wsend, wrecv, send, extra, recv, isend, irecv, dsend, drecv, freed, ready, wrap):
    t, d = x.shape
    r = t // 2
    nl = g_ref.shape[0]
    nloc = nl - 1
    hkv, dh = q.shape[0] // 2, q.shape[2] // 2
    nd = d // 256
    half = nd // 2
    wqb = WKV + nd * hkv
    nz = cp // 2
    i = lax.axis_index('cp')
    c = lax.rem(i, 2)
    z = lax.div(i, 2)
    partner = i + 1 - 2 * c
    up, down = lax.rem(i + 2, cp), lax.rem(i + cp - 2, cp)
    last = z == nz - 1
    scale = dh ** -0.5 * math.log2(math.e)
    h3 = hkv - 1

    lead, follow = c, 1 - c

    def dev(s):
        return jnp.where(s == 0, up, down)

    def nxt(s):
        return jnp.where(s == 0, z + 1 < nz, z > 0)

    def need(s, k):
        return (s == 1) | (z >= k)

    def sl(par, s, p, h):
        return NEAR + ((par * 2 + s) * hkv + h) * 2 + p if p < 2 else FAR + (s * hkv + h) * 2 + p - 2

    def own(s, h):
        return OWN + s * hkv + h

    def rsem(par, s, p, h):
        return recv.at[((par * 2 + s) * 4 + p) * hkv + h]

    def copy(kind, s, h, par):
        src = own(s, h) if kind in (0, 2) else sl(par, s, 3 if kind == 5 else 1, h)
        p = (1, 3, 0, 0, 2, 2)[kind]
        to = dev(s) if kind < 2 else partner
        return _remote(pool.at[src], pool.at[sl(par, s, p, h)], send.at[(kind * 2 + s) * hkv + h], rsem(par, s, p, h), to)

    def cond(kind, s):
        return (nxt(s), nxt(s) & need(s, 1), z >= 0, need(s, 1), need(s, 1), need(s, 2))[kind]

    def start(kind, s, h, par):
        pl.when(cond(kind, s))(lambda: copy(kind, s, h, par).start())

    def edge_copy(h, par):
        return _remote(pool.at[own(0, h)], pool.at[sl(par, 1, 1, h)], extra.at[h], rsem(par, 1, 1, h), partner)

    def arrived(s, p, h, par, when):
        ref = pool.at[sl(par, s, p, h)]
        pl.when(when)(lambda: pltpu.make_async_copy(ref, ref, rsem(par, s, p, h)).wait())

    def raw(kv, l, j):
        rows = pl.ds(pl.multiple_of((c * half + j) * 2048, 2048), 2048)
        slot = lax.rem(j, STAGES)
        if kv:
            return (pltpu.make_async_copy(wk_hbm.at[l, rows], stage.at[slot, :, pl.ds(0, 128)], ssem.at[slot]),
                    pltpu.make_async_copy(wv_hbm.at[l, rows], stage.at[slot, :, pl.ds(128, 128)], ssem.at[STAGES + slot]))
        return (pltpu.make_async_copy(wq_hbm.at[l, rows], stage.at[slot], ssem.at[slot]),)

    def prefetch(kv, l):
        for j in range(min(STAGES, half)):
            for cpy in raw(kv, l, j):
                cpy.start()

    def wslot(kv, core, j):
        return (WKV if kv else wqb) + (core * half + j) * hkv

    def share(kv, core, j):
        ref = pool.at[pl.ds(wslot(kv, core, j), hkv)]
        k = j if kv else half + j
        return _remote(ref, ref, wsend.at[k], wrecv.at[k], partner)

    def shared(kv):
        def one(j):
            ref = pool.at[pl.ds(wslot(kv, 1 - c, j), hkv)]
            pltpu.make_async_copy(ref, ref, wrecv.at[j if kv else half + j]).wait()
            share(kv, c, j).wait_send()

        _for(half, one)

    def relayout(kv, l, wait):
        def chunk(j):
            for cpy in raw(kv, l, j):
                cpy.wait()
            slot = lax.rem(j, STAGES)
            base = wslot(kv, c, j)
            perm = pkv[...] if kv else pq[...]
            for b in range(8):
                out = _dot(perm, stage[slot, b * 256:(b + 1) * 256, :]).astype(BF16)
                rows = slice(b * 32, (b + 1) * 32)
                for a in range(8):
                    part = out[a * 32:(a + 1) * 32]
                    if kv:
                        lane = (a % 2) * 128
                        pool[base + a // 2, rows, lane:lane + 128] = part[:, :128]
                        pool[base + a // 2, rows, dh + lane:dh + lane + 128] = part[:, 128:]
                    else:
                        pool[base + a // 2, rows, (a % 2) * dh:(a % 2 + 1) * dh] = part

            @pl.when(j + STAGES < half)
            def _():
                for cpy in raw(kv, l, j + STAGES):
                    cpy.start()

            @pl.when(j > 0)
            def _():
                share(kv, c, j - 1).start()

        if wait:
            pl.semaphore_wait(freed.at[0 if kv else 1], 1)
        _for(half, chunk)
        share(kv, c, half - 1).start()

    def release(kv):
        pl.semaphore_signal(freed.at[0 if kv else 1], inc=1, device_id={'cp': partner}, device_id_type=MESH)

    def weights(kv, h):
        base = WKV if kv else wqb
        return jnp.concatenate([pool[base + j * hkv + h] for j in range(nd)], axis=0)

    def wo_copy(l, h):
        slot = lax.rem(h, 2)
        return pltpu.make_async_copy(wo_hbm.at[l, pl.ds(pl.multiple_of(h * 2 * dh, 2 * dh), 2 * dh)], wo.at[slot], wosem.at[slot])

    def rows_of(s):
        return pl.ds(pl.multiple_of(s * r, r), r)

    def norm(s, l):
        g = gs[pl.ds(l, 1), :]

        def blk(rows):
            v = x[rows, :].astype(BF16).astype(F32)
            x[rows, :] = v
            m = lax.rsqrt(jnp.mean(v * v, axis=-1, keepdims=True) + EPS)
            n[rows, :] = (v * m * g).astype(BF16)

        _blocks(s * r, r, blk)

    def out_proj(s, slot):
        rows = rows_of(s)
        nb = min(512, d)
        for j in range(d // nb):
            cols = slice(j * nb, (j + 1) * nb)
            x[rows, cols] += _dot(o[rows, :], wo[slot, :, cols])

    def turn(a):
        return _dot_nt(eye[...], a).astype(BF16)

    load_x = pltpu.make_async_copy(x_hbm, n, msem.at[0])
    prefetch(True, 0)
    load_x.start()

    @pl.when(z < 2)
    def _():
        def clear(j):
            pool[NEAR + lax.div(j, 2 * hkv) * 4 * hkv + lax.rem(j, 2 * hkv)] = jnp.zeros(pool.shape[1:], BF16)

        def clear_far(j):
            pool[FAR + j] = jnp.zeros(pool.shape[1:], BF16)

        _for(4 * hkv, clear)
        _for(2 * hkv, clear_far)

    ro = lax.broadcasted_iota(jnp.int32, (256, 256), 0)
    co = lax.broadcasted_iota(jnp.int32, (256, 256), 1)
    pq[...] = jnp.where(co == (ro % 32) * 8 + ro // 32, 1.0, 0.0).astype(BF16)
    pkv[...] = jnp.where(co == (ro % 32) * 8 + ((ro // 32) % 2) * 4 + ro // 64, 1.0, 0.0).astype(BF16)
    eye[...] = jnp.where(ro == co, 1.0, 0.0).astype(BF16)
    for l in range(nl):
        gs[l:l + 1, :] = g_ref[l:l + 1, :].astype(F32)

    bar = pltpu.get_barrier_semaphore()
    for nb in (up, down, partner):
        pl.semaphore_signal(bar, inc=1, device_id={'cp': nb}, device_id_type=MESH)
    pl.semaphore_wait(bar, 3)

    rows2 = lax.broadcasted_iota(jnp.int32, (2 * r, r), 0) % r
    cols2 = lax.broadcasted_iota(jnp.int32, (2 * r, r), 1)

    def put_o(s, out0, out1):
        rows = rows_of(s)
        o[rows, :dh] = out0
        o[rows, dh:] = out1

    def attend(s, h, par):
        qi = s * hkv + h
        qv = jnp.concatenate([q[qi, :, :dh], q[qi, :, dh:]], axis=0)
        a = [own(s, h)] + [sl(par, s, p, h) for p in range(4)]
        sn = _dot_nt(qv, pool[pl.ds(a[1], 2), :, :dh].reshape(2 * r, dh))
        sf = _dot_nt(qv, pool[pl.ds(a[3], 2), :, :dh].reshape(2 * r, dh))
        sc = [jnp.where(cols2 <= rows2, _dot_nt(qv, pool[a[0], :, :dh]), NEG), sn[:, :r], sn[:, r:],
              sf[:, :r], jnp.where(cols2 > rows2, sf[:, r:], NEG)]
        for b in range(1, 5):
            sc[b] = sc[b] + jnp.where((s == 1) | (i >= b), 0.0, NEG).astype(F32)
        m = functools.reduce(jnp.maximum, sc).max(axis=1, keepdims=True)
        pr = [jnp.exp2((v - m) * scale) for v in sc]
        den = functools.reduce(jnp.add, pr).sum(axis=1, keepdims=True)
        num = functools.reduce(jnp.add, [_dot(v.astype(BF16), pool[b, :, dh:]) for v, b in zip(pr, a)])
        out = (num / den).astype(BF16)
        put_o(s, out[:r], out[r:])

    def local_send(s, is_lead, h, par):
        start(0, s, h, par)
        if is_lead:
            start(2, s, h, par)
        pl.when(last & (s == 0))(lambda: edge_copy(h, par).start())

    def drain(s, is_lead, h, par):
        for kind in (0, 1, 2, 4) if is_lead else (0, 1, 3, 5):
            pl.when(cond(kind, s))(lambda k=kind: copy(k, s, h, par).wait_send())
        pl.when(last & (s == 0))(lambda: edge_copy(h, par).wait_send())

    def mine(s, k, h):
        return _pick(k, own(s, h), sl(1, s, 1, h), sl(1, s, 3, h), WKV + ((k - 3) * 2 + s) * 2 * hkv + h * 2)

    def theirs(s, k, h):
        return _pick(k, sl(1, s, 0, h), sl(1, s, 2, h), sl(0, s, 0, h), WKV + ((k - 3) * 2 + s) * 2 * hkv + h * 2 + 1)

    def has(s, k):
        return jnp.where(s == 0, k < nz, z + k < nz)

    def sends(s, k):
        return jnp.where(s == 0, k < nz - 1, (z + k < nz) & (z > 0))

    def sidx(s, k, h):
        return (s * nz + k) * hkv + h

    def ici(s, k, h):
        return _remote(pool.at[mine(s, k, h)], pool.at[mine(s, k + 1, h)], isend.at[sidx(s, k, h)], irecv.at[sidx(s, k + 1, h)],
                       dev(s))

    def d2d(s, k, h):
        return _remote(pool.at[mine(s, k, h)], pool.at[theirs(s, k, h)], dsend.at[sidx(s, k, h)], drecv.at[sidx(s, k, h)], partner)

    def push(s, k, h):
        pl.when(sends(s, k))(lambda: ici(s, k, h).start())
        pl.when(has(s, k))(lambda: d2d(s, k, h).start())

    def got_ici(s, k, h):
        ref = pool.at[mine(s, k, h)]
        pl.when(has(s, k))(lambda: pltpu.make_async_copy(ref, ref, irecv.at[sidx(s, k, h)]).wait())

    def got_d2d(s, k, h):
        ref = pool.at[theirs(s, k, h)]
        pl.when(has(s, k))(lambda: pltpu.make_async_copy(ref, ref, drecv.at[sidx(s, k, h)]).wait())

    def global_kv(s, h, y):
        pool[own(s, h), :, :dh] = y[:, :dh]
        pool[own(s, h), :, dh:] = turn(y[:, dh:])
        push(s, 0, h)

    roles = ((follow, False), (lead, True))

    relayout(True, 0, False)
    load_x.wait()
    _blocks(0, t, lambda rows: x.__setitem__((rows, slice(None)), n[rows, :].astype(F32)))
    norm(follow, 0)
    prefetch(False, 0)
    shared(True)
    for s, is_lead in roles:
        if is_lead:
            norm(s, 0)
        pool[own(s, 0)] = _dot(n[rows_of(s), :], weights(True, 0)).astype(BF16)
        local_send(s, is_lead, 0, 0)
    wo_copy(0, 0).start()
    wo_copy(0, 1).start()

    def layer(l):
        par = lax.rem(l, 2)

        @pl.when((l == nloc - 1) & (z == 0))
        def _():
            pl.semaphore_signal(wrap, inc=1, device_id={'cp': down}, device_id_type=MESH)

        def kv_head(j):
            h = j + 1
            y = _dot(n[...], weights(True, h)).astype(BF16)
            for s in range(2):
                pool[own(s, h)] = y[s * r:(s + 1) * r]
            for s, is_lead in roles:
                local_send(s, is_lead, h, par)

        _for(hkv - 1, kv_head)
        release(True)

        @pl.when(l == 0)
        def _():
            relayout(False, 0, False)

        prefetch(True, l + 1)
        shared(False)

        def q_group(h):
            y = _dot(n[...], weights(False, h)).astype(BF16)
            for s in range(2):
                q[s * hkv + h] = y[s * r:(s + 1) * r]

        _for(hkv, q_group)
        release(False)

        def forward(h):
            for s, is_lead in roles:
                arrived(s, 1, h, par, need(s, 1))
            arrived(follow, 0, h, par, z >= 0)
            for s, is_lead in roles:
                for kind in (1, 4) if is_lead else (1, 3):
                    start(kind, s, h, par)

        forward(0)
        relayout(True, l + 1, True)
        prefetch(False, l + 1)
        forward(1)
        relayout(False, l + 1, True)
        forward(2)
        forward(3)
        shared(True)

        def edge(h):
            for p, core in ((2, 1), (0, 0)):
                @pl.when(last & (c == core))
                def _():
                    arrived(0, p, h, par, z >= 0)
                    pltpu.make_async_copy(pool.at[sl(par, 0, p, h)], pool.at[sl(par, 1, 3, h)], rsem(par, 1, 3, h)).start()

        def gather(s, is_lead, h):
            at_edge = last & (s == 0)
            arrived(s, 3, h, par, need(s, 2))
            if is_lead:
                arrived(s, 0, h, par, need(s, 1) & ~at_edge)
                arrived(s, 2, h, par, need(s, 2))
            else:
                start(5, s, h, par)
                arrived(s, 2, h, par, need(s, 1) & ~at_edge)

        def next_wo(h):
            wrap = lax.div(h + 2, hkv)
            wo_copy(l + wrap, h + 2 - hkv * wrap).start()

        def head(h):
            edge(h)
            for s, is_lead in roles:
                gather(s, is_lead, h)
                attend(s, h, par)
                if not is_lead:
                    wo_copy(l, h).wait()
                out_proj(s, lax.rem(h, 2))
            next_wo(h)

        _for(hkv - 1, head)
        wo_copy(l, h3).wait()
        edge(h3)
        for s, is_lead in roles:
            gather(s, is_lead, h3)
            attend(s, h3, par)
            out_proj(s, h3 % 2)
            if not is_lead:
                _for(hkv - 1, lambda h: [drain(a, b, h, par) for a, b in roles])
            drain(s, is_lead, h3, par)
            norm(s, l + 1)
            y = _dot(n[rows_of(s), :], weights(True, 0)).astype(BF16)

            @pl.when(l < nloc - 1)
            def _():
                pool[own(s, 0)] = y
                local_send(s, is_lead, 0, 1 - par)

            @pl.when(l == nloc - 1)
            def _():
                if not is_lead:
                    pl.when(last)(lambda: pl.semaphore_wait(wrap, 1))
                global_kv(s, 0, y)
        next_wo(h3)

    _for(nloc, layer)

    def kv_head(j):
        h = j + 1
        y = _dot(n[...], weights(True, h)).astype(BF16)
        for s in range(2):
            global_kv(s, h, y[s * r:(s + 1) * r])

    _for(hkv - 1, kv_head)
    shared(False)

    def q_group(h):
        y = _dot(n[...], weights(False, h)).astype(BF16)
        for s in range(2):
            for g in range(2):
                q[s * hkv + h, :, g * r:(g + 1) * r] = turn(y[s * r:(s + 1) * r, g * dh:(g + 1) * dh])

    _for(hkv, q_group)
    for nb in (up, down, partner):
        pl.semaphore_signal(ready, inc=1, device_id={'cp': nb}, device_id_type=MESH)

    def init(j):
        acc[j] = jnp.zeros(acc.shape[1:], F32)
        ml[j, 0:1, :] = jnp.full((1, 2 * r), NEG, F32)
        ml[j, 1:2, :] = jnp.zeros((1, 2 * r), F32)

    _for(2 * hkv, init)
    pl.semaphore_wait(ready, 3)
    keys = lax.broadcasted_iota(jnp.int32, (r, 2 * r), 0)
    toks = lax.broadcasted_iota(jnp.int32, (r, 2 * r), 1) % r

    def flash(qi, a, b, bias=None):
        qt = q[qi]
        sc = _dot(jnp.concatenate([pool[a, :, :dh], pool[b, :, :dh]], axis=0), qt)
        if bias is not None:
            sc = jnp.concatenate([jnp.where(keys <= toks, sc[:r], NEG), sc[r:] + bias], axis=0)
        old = ml[qi, 0:1, :]
        m = jnp.maximum(old, sc.max(axis=0, keepdims=True))
        f = jnp.exp2((old - m) * scale)
        pr = jnp.exp2((sc - m) * scale)
        ml[qi, 0:1, :] = m
        ml[qi, 1:2, :] = ml[qi, 1:2, :] * f + pr.sum(axis=0, keepdims=True)
        pb = pr.astype(BF16)
        acc[qi] = acc[qi] * f + (_dot(pool[a, :, dh:], pb[:r]) + _dot(pool[b, :, dh:], pb[r:]))

    def step(k, h):
        def job(j):
            qs = jnp.where(j < 2, 1, 0)
            ks = jnp.where(j == 1, 1, 0)
            ok = _pick(j, z >= 0, z + k < nz, z - k >= 0)
            pl.when(ok)(lambda: flash(qs * hkv + h, mine(ks, k, h), theirs(ks, k, h)))

        _for(3, job)

    def first(h):
        bias = [jnp.where(c == a, 0.0, NEG).astype(F32) for a in (1, 0)]
        flash(h, mine(0, 0, h), theirs(0, 0, h), bias[0])
        flash(hkv + h, mine(0, 0, h), theirs(0, 0, h))
        flash(hkv + h, mine(1, 0, h), theirs(1, 0, h), bias[1])

    def finish(h):
        for s in range(2):
            qi = s * hkv + h
            ob = (acc[qi] * (1.0 / ml[qi, 1:2, :])).astype(BF16)
            put_o(s, turn(ob[:, :r]), turn(ob[:, r:]))
        wo_copy(nloc, h).wait()
        for s in range(2):
            out_proj(s, lax.rem(h, 2))
        pl.when(h + 2 < hkv)(lambda: wo_copy(nloc, h + 2).start())

    def unit(u):
        k = lax.div(u, hkv)
        h = lax.rem(u, hkv)
        for s in range(2):
            got_d2d(s, k, h)
        pl.when(k == 0)(lambda: first(h))
        pl.when(k > 0)(lambda: step(k, h))
        pl.when(k == nz - 1)(lambda: finish(h))
        v = jnp.where(k == 0, u + hkv, u + 1)

        @pl.when((k == 0) | ((u >= 2 * hkv - 1) & (v < nz * hkv)))
        def _():
            kv, hv = lax.div(v, hkv), lax.rem(v, hkv)
            for s in range(2):
                got_ici(s, kv, hv)
            for s in range(2):
                push(s, kv, hv)

    _for(nz * hkv, unit)
    _blocks(0, t, lambda rows: n.__setitem__((rows, slice(None)), x[rows, :].astype(BF16)))
    out = pltpu.make_async_copy(n, y_hbm, msem.at[0])
    out.start()

    def drain_all(j):
        k = lax.div(j, hkv)
        h = lax.rem(j, hkv)
        for s in range(2):
            pl.when(sends(s, k))(lambda s=s: ici(s, k, h).wait_send())
            pl.when(has(s, k))(lambda s=s: d2d(s, k, h).wait_send())

    _for(nz * hkv, drain_all)
    out.wait()


def solution(mesh):
    cp = mesh.shape['cp']

    def body(x, g, wq, wk, wv, wo):
        t, d = x.shape
        r = t // 2
        nl = g.shape[0]
        hq, dh = wq.shape[2], wq.shape[3]
        hkv = wk.shape[2]
        nz = cp // 2
        assert (hq, hkv, dh, r, W) == (8, 4, 256, 256, 1024)
        wq2 = wq.reshape(nl, d * hq, dh)
        wk2, wv2 = (a.reshape(nl, d, hkv, 2, dh // 2).transpose(0, 1, 3, 2, 4).reshape(nl, d * hkv * 2, dh // 2) for a in (wk, wv))
        wo2 = wo.reshape(nl, hq * dh, d)
        hbm = pl.BlockSpec(memory_space=pl.ANY)
        sems = pltpu.SemaphoreType.DMA
        slots = WKV + 2 * (d // 256) * hkv
        assert slots >= WKV + (nz - 3) * 4 * hkv
        return pl.pallas_call(
            functools.partial(_kernel, cp),
            out_shape=jax.ShapeDtypeStruct((t, d), BF16),
            in_specs=[hbm, pl.BlockSpec(memory_space=pltpu.VMEM), hbm, hbm, hbm, hbm],
            out_specs=hbm,
            scratch_shapes=[
                pltpu.VMEM((t, d), F32),
                pltpu.VMEM((t, d), BF16),
                pltpu.VMEM((2 * hkv, r, 2 * dh), BF16),
                pltpu.VMEM((slots, r, 2 * dh), BF16),
                pltpu.VMEM((2, 2 * dh, d), BF16),
                pltpu.VMEM((STAGES, 2048, 256), BF16),
                pltpu.VMEM((t, 2 * dh), BF16),
                pltpu.VMEM((2 * hkv, dh, 2 * r), F32),
                pltpu.VMEM((2 * hkv, 8, 2 * r), F32),
                pltpu.VMEM((8, d), F32),
                pltpu.VMEM((256, 256), BF16),
                pltpu.VMEM((256, 256), BF16),
                pltpu.VMEM((256, 256), BF16),
                sems((1,)), sems((2 * STAGES,)), sems((2,)), sems((d // 256,)), sems((d // 256,)),
                sems((6 * 2 * hkv,)), sems((hkv,)), sems((2 * 2 * 4 * hkv,)),
                sems((2 * nz * hkv,)), sems((2 * nz * hkv,)), sems((2 * nz * hkv,)), sems((2 * nz * hkv,)),
                pltpu.SemaphoreType.REGULAR((2,)), pltpu.SemaphoreType.REGULAR, pltpu.SemaphoreType.REGULAR,
            ],
            compiler_params=pltpu.CompilerParams(collective_id=0, has_side_effects=True, vmem_limit_bytes=67043328),
            name='layers',
        )(x, g, wq2, wk2, wv2, wo2)

    spec = P(('dp', 'cp'), None)
    return jax.shard_map(body, mesh=mesh, in_specs=(spec, P(), P(), P(), P(), P()), out_specs=spec, check_vma=False)
```

time: 1590 us -> 468 us (0.29)
  Pallas kernels: 0 us -> 464 us
  local copies, waits for them, and re-layouts: 427 us -> 3.4 us
  matrix products: 403 us -> 0 us
  waiting for transfers between devices: 388 us -> 0 us
  other arithmetic: 219 us -> 0 us
  starting transfers between devices: 124 us -> 0 us
  between operations: 16.1 us -> 0.01 us
    pallas_call x0 -> x1, Pallas kernels: none -> 464 us  [body(): pl.pallas_call(functools.partial(_kernel, cp), out_shape=jax.ShapeDtypeSt...]
    dot_general x48 -> x0, matrix products: 403 us -> none  [the longest x12 139 us: _attend(): jnp.einsum('hgqk,khd->qhgd', p, v, preferred_element_type=jnp.float32)]
    ppermute x40 -> x0, waiting for transfers between devices: 217 us -> none  [the longest x20 128 us: body(): blk_a = lax.ppermute(send_a, 'cp', fwd)]
    unnamed x241 -> x1, local copies, waits for them, and re-layouts: 202 us -> 3.4 us
    sub x15 -> x0, other arithmetic: 176 us -> none  [the longest x12 176 us: _attend(): p = jax.nn.softmax(s, axis=-1).astype(jnp.bfloat16)]
    all_gather x1 -> x0, waiting for transfers between devices: 170 us -> none  [body(): kvg = lax.all_gather(kv, 'cp', axis=1, tiled=True)]
    slice x21 -> x0, local copies, waits for them, and re-layouts: 164 us -> none  [the longest x2 45.5 us: body(): kv = jnp.stack([_proj(n, wk[l]), _proj(n, wv[l])])]
    ppermute x40 -> x0, starting transfers between devices: 124 us -> none  [the longest x20 81.8 us: body(): blk_a = lax.ppermute(send_a, 'cp', fwd)]
  transfers between devices with their start and end apart: 41 -> 0, of which waited for: 29 -> 0; matrix products, arithmetic and copies ran while one was open for 26% -> 0% of each run, Pallas kernels for 0% -> 0%
where the time goes in v3:
time: 468 us; the launch traced here: 467 us
  Pallas kernels  464 us (99%)
    pallas_call x1, Pallas kernels, body(): pl.pallas_call(functools.partial(_kernel, cp), out_shape=jax.ShapeDtypeSt...  464 us

profile of v3, /device:TPU:21, one launch (start us, length us, event | category | flops | bytes accessed | tf_op | source)
XLA Modules:
  0.0 467.4 jit_solution(18307467899695946973)
XLA Ops:
  0.0 464.0 %layers.1 = bf16[512,2560]{1,0:T(8,128)(2,1)} custom-call(bf16[512,2560]{1,0:T(8,128)(2,1)} %x_hbm.1, bf16[6,2560]{1,0:T(8,128)(2,1)} %g_ref.1, bf16[6,20480,256]{2,1,0:T(8,128)(2,1)} %bitcast.12, bf16[6,20480,128]{2,1,0:T(8,128)(2,1)} %bitcast.14, bf16[6,20480,128]{2,1,0:T(8,128)(2,1)} %bitcast.15, bf16[6,2048,2560]{2,1,0:T(8,128)(2,1)} %bitcast.13), custom_call_target="tpu_custom_call" | custom-call | tf_op jit(solution)/shard_map/layers/pallas_call | solution.py:559
  464.0 3.4 copy.10

commit v4 on v3

v4 whole, which is shorter than its diff:
```python
import functools
import math

import jax
import jax.numpy as jnp
from jax import lax
from jax.experimental import pallas as pl
from jax.experimental.pallas import tpu as pltpu
from jax.sharding import PartitionSpec as P

W = 1024
EPS = 1e-6
F32 = jnp.float32
BF16 = jnp.bfloat16
MESH = pl.DeviceIdType.MESH
STAGES = 3
STREAMS = (0, 1)
KV, Q, LEAD, FOLLOW, NO = True, False, True, False, False
TILE, LANES, ROWS = 256, 128, 2048
NEG = float('-inf')

NEAR, FAR, OWN, WKV = 0, 32, 48, 56


def _dot(a, b):
    return jnp.dot(a, b, preferred_element_type=F32)


def _dot_nt(a, b):
    return lax.dot_general(a, b, (((1,), (1,)), ((), ())), preferred_element_type=F32)


def _for(n, body):
    lax.fori_loop(0, n, lambda j, c: (body(j), c)[1], 0)


def _pick(j, *vals):
    out = vals[-1]
    for k in range(len(vals) - 2, -1, -1):
        out = jnp.where(j == k, vals[k], out)
    return out


def _remote(src, dst, ssem, rsem, dev):
    return pltpu.make_async_remote_copy(src_ref=src, dst_ref=dst, send_sem=ssem, recv_sem=rsem,
                                        device_id={'cp': dev}, device_id_type=MESH)


def _blocks(lo, n, body):
    rows = 64

    def blk(j):
        body(pl.ds(pl.multiple_of(lo + j * rows, rows), rows))

    _for(n // rows, blk)


def _kernel(cp, x_hbm, g_ref, wq_hbm, wk_hbm, wv_hbm, wo_hbm, y_hbm,
            x, n, q, pool, wo, stage, o, acc, ml, mask, gs, pq, pkv, eye,
            msem, ssem, wosem, wsend, wrecv, send, extra, recv, isend, irecv, dsend, drecv, freed, ready, wrap, credit):
    t, d = x.shape
    r = t // 2
    nl = g_ref.shape[0]
    nloc = nl - 1
    hkv, dh = q.shape[0] // 2, q.shape[2] // 2
    nd = d // 256
    half = nd // 2
    wqb = WKV + nd * hkv
    nz = cp // 2
    i = lax.axis_index('cp')
    c = lax.rem(i, 2)
    z = lax.div(i, 2)
    partner = i + 1 - 2 * c
    up, down = lax.rem(i + 2, cp), lax.rem(i + cp - 2, cp)
    last = z == nz - 1
    scale = dh ** -0.5 * math.log2(math.e)
    h3 = hkv - 1
    hh = 2 * hkv

    lead, follow = c, 1 - c

    def dev(s):
        return jnp.where(s == 0, up, down)

    def nxt(s):
        return jnp.where(s == 0, z + 1 < nz, z > 0)

    def need(s, k):
        return (s == 1) | (z >= k)

    def sl(par, s, p, h):
        return NEAR + ((par * 2 + s) * hkv + h) * 2 + p if p < 2 else FAR + (s * hkv + h) * 2 + p - 2

    def own(s, h):
        return OWN + s * hkv + h

    def rsem(par, s, p, h):
        return recv.at[((par * 2 + s) * 4 + p) * hkv + h]

    def copy(kind, s, h, par):
        src = own(s, h) if kind in (0, 2) else sl(par, s, 3 if kind == 5 else 1, h)
        p = (1, 3, 0, 0, 2, 2)[kind]
        to = dev(s) if kind < 2 else partner
        return _remote(pool.at[src], pool.at[sl(par, s, p, h)], send.at[(kind * 2 + s) * hkv + h], rsem(par, s, p, h), to)

    def cond(kind, s):
        return (nxt(s), nxt(s) & need(s, 1), z >= 0, need(s, 1), need(s, 1), need(s, 2))[kind]

    def start(kind, s, h, par):
        pl.when(cond(kind, s))(lambda: copy(kind, s, h, par).start())

    def edge_copy(h, par):
        return _remote(pool.at[own(0, h)], pool.at[sl(par, 1, 1, h)], extra.at[h], rsem(par, 1, 1, h), partner)

    def arrived(s, p, h, par, when):
        ref = pool.at[sl(par, s, p, h)]
        pl.when(when)(lambda: pltpu.make_async_copy(ref, ref, rsem(par, s, p, h)).wait())

    def raw(kv, l, j, base):
        rows = pl.ds(pl.multiple_of((base + j) * ROWS, ROWS), ROWS)
        slot = lax.rem(j, STAGES)
        if kv:
            return (pltpu.make_async_copy(wk_hbm.at[l, rows], stage.at[slot, :, pl.ds(0, LANES)], ssem.at[slot]),
                    pltpu.make_async_copy(wv_hbm.at[l, rows], stage.at[slot, :, pl.ds(LANES, LANES)], ssem.at[STAGES + slot]))
        return (pltpu.make_async_copy(wq_hbm.at[l, rows], stage.at[slot], ssem.at[slot]),)

    def prefetch(kv, l, base=c * half, count=half):
        for j in range(min(STAGES, count)):
            for cpy in raw(kv, l, j, base):
                cpy.start()

    def wslot(kv, core, j):
        return (WKV if kv else wqb) + (core * half + j) * hkv

    def share(kv, core, j):
        ref = pool.at[pl.ds(wslot(kv, core, j), hkv)]
        k = j if kv else half + j
        return _remote(ref, ref, wsend.at[k], wrecv.at[k], partner)

    def shared(kv):
        def one(j):
            ref = pool.at[pl.ds(wslot(kv, 1 - c, j), hkv)]
            pltpu.make_async_copy(ref, ref, wrecv.at[j if kv else half + j]).wait()
            share(kv, c, j).wait_send()

        _for(half, one)

    def relayout(kv, l, sharing, first=c * half, count=half):
        def chunk(j):
            for cpy in raw(kv, l, j, first):
                cpy.wait()
            slot = lax.rem(j, STAGES)
            base = (WKV if kv else wqb) + (first + j) * hkv
            perm = pkv[...] if kv else pq[...]
            for b in range(8):
                out = _dot(perm, stage[slot, b * 256:(b + 1) * 256, :]).astype(BF16)
                rows = slice(b * 32, (b + 1) * 32)
                for a in range(8):
                    part = out[a * 32:(a + 1) * 32]
                    if kv:
                        lane = (a % 2) * LANES
                        pool[base + a // 2, rows, lane:lane + LANES] = part[:, :LANES]
                        pool[base + a // 2, rows, dh + lane:dh + lane + LANES] = part[:, LANES:]
                    else:
                        pool[base + a // 2, rows, (a % 2) * dh:(a % 2 + 1) * dh] = part

            @pl.when(j + STAGES < count)
            def _():
                for cpy in raw(kv, l, j + STAGES, first):
                    cpy.start()

            if sharing:
                pl.when(j > 0)(lambda: share(kv, c, j - 1).start())

        _for(count, chunk)
        if sharing:
            share(kv, c, half - 1).start()

    def share_all(kv):
        _for(half, lambda j: share(kv, c, j).start())

    def release(kv):
        pl.semaphore_signal(freed.at[0 if kv else 1], inc=1, device_id={'cp': partner}, device_id_type=MESH)

    def weights(kv, h):
        base = WKV if kv else wqb
        return jnp.concatenate([pool[base + j * hkv + h] for j in range(nd)], axis=0)

    def wo_copy(l, e):
        slot = lax.rem(e, 2)
        rows = pl.ds(pl.multiple_of(lax.rem(e, hkv) * 2 * dh, 2 * dh), 2 * dh)
        return pltpu.make_async_copy(wo_hbm.at[l, rows], wo.at[slot], wosem.at[slot])

    def rows_of(s):
        return pl.ds(pl.multiple_of(s * r, r), r)

    def norm(s, l):
        g = gs[pl.ds(l, 1), :]

        def blk(rows):
            v = x[rows, :].astype(BF16).astype(F32)
            x[rows, :] = v
            m = lax.rsqrt(jnp.mean(v * v, axis=-1, keepdims=True) + EPS)
            n[rows, :] = (v * m * g).astype(BF16)

        _blocks(s * r, r, blk)

    def out_tiles(s, h, slot, nb):
        rows = rows_of(s)

        def tile(j):
            cols = slice(j * nb, (j + 1) * nb)
            x[rows, cols] += _dot(o[lax.rem(h, 2), rows, :], wo[slot, :, cols])

        return [functools.partial(tile, j) for j in range(d // nb)]

    def out_proj(s, h, slot):
        for tile in out_tiles(s, h, slot, min(512, d)):
            tile()

    def turn(a):
        return _dot_nt(eye[...], a).astype(BF16)

    bar = pltpu.get_barrier_semaphore()
    for nb in (up, down, partner):
        pl.semaphore_signal(bar, inc=1, device_id={'cp': nb}, device_id_type=MESH)
    load_x = pltpu.make_async_copy(x_hbm, n, msem.at[0])
    load_x.start()
    prefetch(KV, 0, 0, nd)

    ro = lax.broadcasted_iota(jnp.int32, (TILE, TILE), 0)
    co = lax.broadcasted_iota(jnp.int32, (TILE, TILE), 1)
    pq[...] = jnp.where(co == (ro % 32) * 8 + ro // 32, 1.0, 0.0).astype(BF16)
    pkv[...] = jnp.where(co == (ro % 32) * 8 + ((ro // 32) % 2) * 4 + ro // 64, 1.0, 0.0).astype(BF16)
    eye[...] = jnp.where(ro == co, 1.0, 0.0).astype(BF16)
    mask[0] = jnp.where(co <= ro, 0.0, NEG).astype(F32)
    mask[1] = jnp.where(co > ro, 0.0, NEG).astype(F32)
    for l in range(nl):
        gs[l:l + 1, :] = g_ref[l:l + 1, :].astype(F32)


    def put_o(s, h, out0, out1):
        rows = rows_of(s)
        o[lax.rem(h, 2), rows, :dh] = out0
        o[lax.rem(h, 2), rows, dh:] = out1

    def attend(s, h, par, fill):
        qi = s * hkv + h
        qv = jnp.concatenate([q[qi, :, :dh], q[qi, :, dh:]], axis=0)
        a = [own(s, h)] + [sl(par, s, p, h) for p in range(4)]
        s0 = _dot_nt(qv, pool[a[0], :, :dh])
        sn = _dot_nt(qv, pool[pl.ds(a[1], 2), :, :dh].reshape(t, dh))
        sf = _dot_nt(qv, pool[pl.ds(a[3], 2), :, :dh].reshape(t, dh))
        miss = [jnp.where((s == 1) | (i >= b), 0.0, NEG).astype(F32) for b in range(5)]
        ch = 64
        probs, inv = [], []
        fill = list(fill)
        steps = 2 * r // ch
        for k in range(steps):
            rows = slice(k * ch, (k + 1) * ch)
            lo = k * ch % r
            sc = [s0[rows] + mask[0, lo:lo + ch, :], sn[rows, :r], sn[rows, r:], sf[rows, :r],
                  sf[rows, r:] + mask[1, lo:lo + ch, :]]
            tops = [jnp.maximum(v[:, :LANES], v[:, LANES:]) for v in sc]
            tops = [tops[0]] + [v + miss[b] for b, v in enumerate(tops) if b]
            m = functools.reduce(jnp.maximum, tops).max(axis=1, keepdims=True) * scale
            pr = [jnp.exp2(v * scale - (m - miss[b])) for b, v in enumerate(sc)]
            inv.append(1.0 / functools.reduce(jnp.add, pr).sum(axis=1, keepdims=True))
            probs.append([v.astype(BF16) for v in pr])
            for _ in range(-(-len(fill) // (steps - k))):
                fill.pop(0)()
        pb = [jnp.concatenate([v[b] for v in probs], axis=0) for b in range(5)]
        num = functools.reduce(jnp.add, [_dot(v, pool[b, :, dh:]) for v, b in zip(pb, a)])
        out = (num * jnp.concatenate(inv, axis=0)).astype(BF16)
        put_o(s, h, out[:r], out[r:])

    def local_send(s, is_lead, h, par):
        start(0, s, h, par)
        if is_lead:
            start(2, s, h, par)
        pl.when(last & (s == 0))(lambda: edge_copy(h, par).start())

    def drain(s, is_lead, h, par):
        for kind in (0, 1, 2, 4) if is_lead else (0, 1, 3, 5):
            pl.when(cond(kind, s))(lambda k=kind: copy(k, s, h, par).wait_send())
        pl.when(last & (s == 0))(lambda: edge_copy(h, par).wait_send())

    def mine(s, k, h):
        return _pick(k, own(s, h), sl(1, s, 1, h), sl(1, s, 3, h), WKV + ((k - 3) * 2 + s) * hh + h * 2)

    def theirs(s, k, h):
        return _pick(k, sl(1, s, 0, h), sl(1, s, 2, h), sl(0, s, 0, h), WKV + ((k - 3) * 2 + s) * hh + h * 2 + 1)

    def has(s, k):
        return jnp.where(s == 0, k < nz, z + k < nz)

    def sends(s, k):
        return jnp.where(s == 0, k < nz - 1, (z + k < nz) & (z > 0))

    def sidx(s, k, h):
        return (s * nz + k) * hkv + h

    def ici(s, k, h):
        return _remote(pool.at[mine(s, k, h)], pool.at[mine(s, k + 1, h)], isend.at[sidx(s, k, h)], irecv.at[sidx(s, k + 1, h)],
                       dev(s))

    def d2d(s, k, h):
        return _remote(pool.at[mine(s, k, h)], pool.at[theirs(s, k, h)], dsend.at[sidx(s, k, h)], drecv.at[sidx(s, k, h)], partner)

    def push(s, k, h):
        pl.when(sends(s, k))(lambda: ici(s, k, h).start())
        pl.when(has(s, k))(lambda: d2d(s, k, h).start())

    def got_ici(s, k, h):
        ref = pool.at[mine(s, k, h)]
        pl.when(has(s, k))(lambda: pltpu.make_async_copy(ref, ref, irecv.at[sidx(s, k, h)]).wait())

    def got_d2d(s, k, h):
        ref = pool.at[theirs(s, k, h)]
        pl.when(has(s, k))(lambda: pltpu.make_async_copy(ref, ref, drecv.at[sidx(s, k, h)]).wait())

    def global_kv(s, h, y):
        pool[own(s, h), :, :dh] = y[:, :dh]
        pool[own(s, h), :, dh:] = turn(y[:, dh:])
        push(s, 0, h)

    roles = ((follow, FOLLOW), (lead, LEAD))

    def local_keys(s, is_lead, par):
        def one(h):
            pool[own(s, h)] = _dot(n[rows_of(s), :], weights(KV, h)).astype(BF16)
            local_send(s, is_lead, h, par)

        _for(hkv, one)

    def global_keys(s):
        _for(hkv, lambda h: global_kv(s, h, _dot(n[rows_of(s), :], weights(KV, h)).astype(BF16)))

    def forward(is_lead, h, l, par):
        s = lead if is_lead else follow
        arrived(s, 1, h, par, need(s, 1))
        if is_lead:
            arrived(follow, 0, h, par, z >= 0)
        pl.when((h == 0) & (l > 0) & cond(1, s))(lambda: pl.semaphore_wait(credit.at[int(is_lead)], 1))
        for kind in (1, 4) if is_lead else (1, 3):
            start(kind, s, h, par)

    def relay_early(h):
        got_ici(follow, 1, h)
        pl.when((h == 0) & sends(follow, 1))(lambda: pl.semaphore_wait(credit.at[0], 1))
        pl.when(sends(follow, 1))(lambda: ici(follow, 1, h).start())

    def give_credit(is_lead, final):
        s = lead if is_lead else follow
        giver = jnp.where(s == 0, final | (z >= 2), jnp.where(final, z + 2 < nz, z + 1 < nz))

        @pl.when(giver)
        def _():
            to = jnp.where(s == 0, down, up)
            pl.semaphore_signal(credit.at[int(is_lead)], inc=1, device_id={'cp': to}, device_id_type=MESH)

    def clear():
        def one(h):
            for p, when in enumerate(((z == 0) & (c == 0), z == 0, (z == 0) | ((z == 1) & (c == 0)), z < 2)):
                for par in range(2 if p < 2 else 1):
                    pl.when(when)(lambda p=p, par=par: pool.__setitem__(sl(par, 0, p, h), jnp.zeros(pool.shape[1:], BF16)))

        _for(hkv, one)

    with jax.named_scope('entry_x'):
        load_x.wait()
        _blocks(0, t, lambda rows: x.__setitem__((rows, slice(None)), n[rows, :].astype(F32)))
        norm(follow, 0)
    with jax.named_scope('entry_kv'):
        relayout(KV, 0, NO, 0, nd)
        prefetch(Q, 0)
        wo_copy(0, 0).start()
        wo_copy(0, 1).start()
    with jax.named_scope('entry_barrier'):
        pl.semaphore_wait(bar, 3)
    with jax.named_scope('entry_keys_f'):
        local_keys(follow, FOLLOW, 0)
    with jax.named_scope('entry_q'):
        relayout(Q, 0, True)
    with jax.named_scope('entry_keys_l'):
        norm(lead, 0)
        pl.when(z < 2)(clear)
        for h in range(h3):
            forward(FOLLOW, h, 0, 0)
        local_keys(lead, LEAD, 0)
        release(KV)

    def layer(l):
        par = lax.rem(l, 2)
        final = l == nloc - 1

        @pl.when(final & (z == 0))
        def _():
            pl.semaphore_signal(wrap, inc=1, device_id={'cp': down}, device_id_type=MESH)

        with jax.named_scope('q'):
            prefetch(KV, l + 1)
            shared(Q)

            def q_group(h):
                y = _dot(n[...], weights(Q, h)).astype(BF16)
                for s in STREAMS:
                    q[s * hkv + h] = y[s * r:(s + 1) * r]

            _for(hkv, q_group)
            release(Q)
        with jax.named_scope('forward_a'):
            forward(FOLLOW, h3, l, par)
            forward(LEAD, 0, l, par)
        with jax.named_scope('relayout_kv'):
            pl.semaphore_wait(freed.at[0], 1)
            relayout(KV, l + 1, True)
            prefetch(Q, l + 1)

        def edge(h):
            for p, core in ((2, 1), (0, 0)):
                @pl.when(last & (c == core))
                def _():
                    arrived(0, p, h, par, z >= 0)
                    pltpu.make_async_copy(pool.at[sl(par, 0, p, h)], pool.at[sl(par, 1, 3, h)], rsem(par, 1, 3, h)).start()

        def gather(s, is_lead, h):
            at_edge = last & (s == 0)
            if not is_lead:
                edge(h)
            arrived(s, 3, h, par, need(s, 2))
            if is_lead:
                arrived(s, 0, h, par, need(s, 1) & ~at_edge)
                arrived(s, 2, h, par, need(s, 2))
            else:
                start(5, s, h, par)
                arrived(s, 2, h, par, need(s, 1) & ~at_edge)

        def use(is_lead, h):
            return h + (hkv if is_lead else 0)

        def next_wo(e):
            wrapped = lax.div(e + 2, hh)
            wo_copy(l + wrapped, e + 2 - hh * wrapped).start()

        def head(s, is_lead, h, first):
            with jax.named_scope('gather'):
                gather(s, is_lead, h)
                if not first:
                    wo_copy(l, use(is_lead, h - 1)).wait()
            with jax.named_scope('attend'):
                attend(s, h, par, [] if first else out_tiles(s, h - 1, lax.rem(h - 1, 2), 256))
            if not first:
                next_wo(use(is_lead, h - 1))

        def heads(s, is_lead, after):
            head(s, is_lead, 0, True)
            after(0)

            def one(j):
                head(s, is_lead, j + 1, False)
                after(j + 1)

            _for(h3, one)

        def tail(s, is_lead):
            with jax.named_scope('out'):
                wo_copy(l, use(is_lead, h3)).wait()
                out_proj(s, h3, h3 % 2)
                next_wo(use(is_lead, h3))
            with jax.named_scope('norm'):
                norm(s, l + 1)
            with jax.named_scope('drain'):
                _for(hkv, lambda h: drain(s, is_lead, h, par))
                if is_lead:
                    pl.when(~final)(lambda: give_credit(is_lead, False))
                else:
                    give_credit(is_lead, final)
            with jax.named_scope('keys'):
                @pl.when(~final)
                def _():
                    local_keys(s, is_lead, 1 - par)

                @pl.when(final)
                def _():
                    if not is_lead:
                        pl.when(last)(lambda: pl.semaphore_wait(wrap, 1))
                    global_keys(s)

        def ahead(h):
            pl.when(~final)(lambda: forward(FOLLOW, h, l + 1, 1 - par))
            pl.when(final)(lambda: relay_early(h))

        def after_f(h):
            pl.when(h == 0)(lambda: forward(LEAD, 1, l, par))

            @pl.when(h == 1)
            def _():
                relayout(Q, l + 1, NO)
                forward(LEAD, 2, l, par)
                forward(LEAD, 3, l, par)
                shared(KV)

        def after_l(h):
            pl.when(h == 1)(lambda: ahead(0))
            pl.when(h == 2)(lambda: ahead(1))

        heads(follow, FOLLOW, after_f)
        pl.semaphore_wait(freed.at[1], 1)
        share_all(Q)
        tail(follow, FOLLOW)
        heads(lead, LEAD, after_l)
        ahead(2)
        tail(lead, LEAD)
        pl.when(~final)(lambda: release(KV))

    _for(nloc, layer)

    shared(Q)

    def q_group(h):
        y = _dot(n[...], weights(Q, h)).astype(BF16)
        for s in STREAMS:
            for g in range(2):
                q[s * hkv + h, :, g * r:(g + 1) * r] = turn(y[s * r:(s + 1) * r, g * dh:(g + 1) * dh])

    _for(hkv, q_group)
    for nb in (up, down, partner):
        pl.semaphore_signal(ready, inc=1, device_id={'cp': nb}, device_id_type=MESH)

    def init(j):
        acc[j] = jnp.zeros(acc.shape[1:], F32)
        ml[j, 0:1, :] = jnp.full((1, t), NEG, F32)
        ml[j, 1:2, :] = jnp.zeros((1, t), F32)

    _for(hh, init)
    pl.semaphore_wait(ready, 3)

    def relay(s, k, h):
        got_ici(s, k, h)
        push(s, k, h)

    relay_early(h3)
    _for(hkv, lambda h: pl.when(has(follow, 1))(lambda: d2d(follow, 1, h).start()))
    keys = lax.broadcasted_iota(jnp.int32, (r, t), 0)
    toks = lax.broadcasted_iota(jnp.int32, (r, t), 1) % r

    def flash(qi, a, b, bias=None):
        qt = q[qi]
        sc = _dot(jnp.concatenate([pool[a, :, :dh], pool[b, :, :dh]], axis=0), qt)
        if bias is not None:
            sc = jnp.concatenate([jnp.where(keys <= toks, sc[:r], NEG), sc[r:] + bias], axis=0)
        old = ml[qi, 0:1, :]
        m = jnp.maximum(old, sc.max(axis=0, keepdims=True))
        f = jnp.exp2((old - m) * scale)
        pr = jnp.exp2((sc - m) * scale)
        ml[qi, 0:1, :] = m
        ml[qi, 1:2, :] = ml[qi, 1:2, :] * f + pr.sum(axis=0, keepdims=True)
        pb = pr.astype(BF16)
        acc[qi] = acc[qi] * f + (_dot(pool[a, :, dh:], pb[:r]) + _dot(pool[b, :, dh:], pb[r:]))

    def step(k, h):
        def job(j):
            qs = jnp.where(j < 2, 1, 0)
            ks = jnp.where(j == 1, 1, 0)
            ok = _pick(j, z >= 0, z + k < nz, z - k >= 0)
            pl.when(ok)(lambda: flash(qs * hkv + h, mine(ks, k, h), theirs(ks, k, h)))

        _for(3, job)

    def first(h):
        bias = [jnp.where(c == a, 0.0, NEG).astype(F32) for a in (1, 0)]
        flash(h, mine(0, 0, h), theirs(0, 0, h), bias[0])
        flash(hkv + h, mine(0, 0, h), theirs(0, 0, h))
        flash(hkv + h, mine(1, 0, h), theirs(1, 0, h), bias[1])

    def finish_o(s, h):
        qi = s * hkv + h
        ob = (acc[qi] * (1.0 / ml[qi, 1:2, :])).astype(BF16)
        put_o(s, h, turn(ob[:, :r]), turn(ob[:, r:]))

    def finish(h):
        for s in STREAMS:
            finish_o(s, h)
        wo_copy(nloc, h).wait()
        for s in STREAMS:
            out_proj(s, h, lax.rem(h, 2))
        pl.when(h + 2 < hkv)(lambda: wo_copy(nloc, h + 2).start())

    def put(rows):
        n[rows, :] = x[rows, :].astype(BF16)
        pltpu.make_async_copy(n.at[rows], y_hbm.at[rows], msem.at[0]).start()

    def drain_unit(j):
        k, h = lax.div(j, hkv), lax.rem(j, hkv)
        for s in STREAMS:
            pl.when(sends(s, k))(lambda s=s: ici(s, k, h).wait_send())
            pl.when(has(s, k))(lambda s=s: d2d(s, k, h).wait_send())

    def ready_keys(k, h):
        with jax.named_scope('got'):
            for s in STREAMS:
                got_d2d(s, k, h)

    def unit(u):
        k = lax.div(u, hkv)
        h = lax.rem(u, hkv)
        ready_keys(k, h)
        with jax.named_scope('flash'):
            pl.when(k == 0)(lambda: first(h))
            pl.when(k > 0)(lambda: step(k, h))
        with jax.named_scope('finish'):
            pl.when(k == nz - 1)(lambda: finish(h))
            pl.when(k > 1)(lambda: drain_unit(u - hh))
        pl.when(k == 0)(lambda: relay(lead, 1, h))
        v = u + 1

        @pl.when((v >= hh) & (v < nz * hkv))
        def _():
            for s in STREAMS:
                relay(s, lax.div(v, hkv), lax.rem(v, hkv))

    units = nz * hkv
    with jax.named_scope('units'):
        _for(units - 1, unit)
    _for(hkv + 1, lambda j: drain_unit(units - hh - 1 + j))
    wo_copy(nloc, h3).wait()
    ready_keys(nz - 1, h3)
    with jax.named_scope('flash'):
        step(nz - 1, h3)
    with jax.named_scope('end'):
        for s in STREAMS:
            finish_o(s, h3)
        for s in STREAMS:
            out_proj(s, h3, h3 % 2)
            _blocks(s * r, r, put)
        _for(hkv, lambda j: drain_unit(units - hkv + j))
        pltpu.make_async_copy(n, y_hbm, msem.at[0]).wait()


def solution(mesh):
    cp = mesh.shape['cp']

    def body(x, g, wq, wk, wv, wo):
        t, d = x.shape
        r = t // 2
        nl = g.shape[0]
        hq, dh = wq.shape[2], wq.shape[3]
        hkv = wk.shape[2]
        nz = cp // 2
        assert (hq, hkv, dh, r, W) == (8, 4, 256, 256, 1024)
        wq2 = wq.reshape(nl, d * hq, dh)
        wk2, wv2 = (a.reshape(nl, d, hkv, 2, dh // 2).transpose(0, 1, 3, 2, 4).reshape(nl, d * hkv * 2, dh // 2) for a in (wk, wv))
        wo2 = wo.reshape(nl, hq * dh, d)
        hbm = pl.BlockSpec(memory_space=pl.ANY)
        sems = pltpu.SemaphoreType.DMA
        slots = WKV + 2 * (d // 256) * hkv
        assert slots >= WKV + (nz - 3) * 4 * hkv
        return pl.pallas_call(
            functools.partial(_kernel, cp),
            out_shape=jax.ShapeDtypeStruct((t, d), BF16),
            in_specs=[hbm, pl.BlockSpec(memory_space=pltpu.VMEM), hbm, hbm, hbm, hbm],
            out_specs=hbm,
            scratch_shapes=[
                pltpu.VMEM((t, d), F32),
                pltpu.VMEM((t, d), BF16),
                pltpu.VMEM((2 * hkv, r, 2 * dh), BF16),
                pltpu.VMEM((slots, r, 2 * dh), BF16),
                pltpu.VMEM((2, 2 * dh, d), BF16),
                pltpu.VMEM((STAGES, ROWS, 256), BF16),
                pltpu.VMEM((2, t, 2 * dh), BF16),
                pltpu.VMEM((2 * hkv, dh, 2 * r), F32),
                pltpu.VMEM((2 * hkv, 8, 2 * r), F32),
                pltpu.VMEM((2, r, r), F32),
                pltpu.VMEM((8, d), F32),
                pltpu.VMEM((TILE, TILE), BF16),
                pltpu.VMEM((TILE, TILE), BF16),
                pltpu.VMEM((TILE, TILE), BF16),
                sems((1,)), sems((2 * STAGES,)), sems((2,)), sems((d // 256,)), sems((d // 256,)),
                sems((6 * 2 * hkv,)), sems((hkv,)), sems((2 * 2 * 4 * hkv,)),
                sems((2 * nz * hkv,)), sems((2 * nz * hkv,)), sems((2 * nz * hkv,)), sems((2 * nz * hkv,)),
                pltpu.SemaphoreType.REGULAR((2,)), pltpu.SemaphoreType.REGULAR, pltpu.SemaphoreType.REGULAR,
                pltpu.SemaphoreType.REGULAR((2,)),
            ],
            compiler_params=pltpu.CompilerParams(collective_id=0, has_side_effects=True, vmem_limit_bytes=67043328),
            name='layers',
        )(x, g, wq2, wk2, wv2, wo2)

    spec = P(('dp', 'cp'), None)
    return jax.shard_map(body, mesh=mesh, in_specs=(spec, P(), P(), P(), P(), P()), out_specs=spec, check_vma=False)
```

time: 468 us -> 420 us (0.90)
  Pallas kernels: 464 us -> 416 us
    pallas_call x1, Pallas kernels: 464 us -> 416 us  [body(): pl.pallas_call(functools.partial(_kernel, cp), out_shape=jax.ShapeDtypeSt...]
where the time goes in v4:
time: 420 us; the launch traced here: 419 us
  Pallas kernels  416 us (99%)
    pallas_call x1, Pallas kernels, body(): pl.pallas_call(functools.partial(_kernel, cp), out_shape=jax.ShapeDtypeSt...  416 us

profile of v4, /device:TPU:21, one launch (start us, length us, event | category | flops | bytes accessed | tf_op | source)
XLA Modules:
  0.0 419.4 jit_solution(5769453959991992359)
XLA Ops:
  0.0 416.0 %layers.1 = bf16[512,2560]{1,0:T(8,128)(2,1)} custom-call(bf16[512,2560]{1,0:T(8,128)(2,1)} %x_hbm.1, bf16[6,2560]{1,0:T(8,128)(2,1)} %g_ref.1, bf16[6,20480,256]{2,1,0:T(8,128)(2,1)} %bitcast.12, bf16[6,20480,128]{2,1,0:T(8,128)(2,1)} %bitcast.14, bf16[6,20480,128]{2,1,0:T(8,128)(2,1)} %bitcast.15, bf16[6,2048,2560]{2,1,0:T(8,128)(2,1)} %bitcast.13), custom_call_target="tpu_custom_call" | custom-call | tf_op jit(solution)/shard_map/layers/pallas_call | solution.py:659
  416.0 3.4 copy.10

commit v5 on v4

--- a/solution.py
+++ b/solution.py
@@ -382,6 +382,7 @@
         local_keys(follow, FOLLOW, 0)
     with jax.named_scope('entry_q'):
         relayout(Q, 0, True)
+        prefetch(KV, 1)
     with jax.named_scope('entry_keys_l'):
         norm(lead, 0)
         pl.when(z < 2)(clear)
@@ -398,8 +399,11 @@
         def _():
             pl.semaphore_signal(wrap, inc=1, device_id={'cp': down}, device_id_type=MESH)
 
+        with jax.named_scope('relayout_kv'):
+            pl.semaphore_wait(freed.at[0], 1)
+            relayout(KV, l + 1, True)
+            prefetch(Q, l + 1)
         with jax.named_scope('q'):
-            prefetch(KV, l + 1)
             shared(Q)
 
             def q_group(h):
@@ -412,10 +416,10 @@
         with jax.named_scope('forward_a'):
             forward(FOLLOW, h3, l, par)
             forward(LEAD, 0, l, par)
-        with jax.named_scope('relayout_kv'):
-            pl.semaphore_wait(freed.at[0], 1)
-            relayout(KV, l + 1, True)
-            prefetch(Q, l + 1)
+        with jax.named_scope('relayout_q'):
+            relayout(Q, l + 1, NO)
+            pl.when(l + 2 < nl)(lambda: prefetch(KV, l + 2))
+            forward(LEAD, 1, l, par)
 
         def edge(h):
             for p, core in ((2, 1), (0, 0)):
@@ -492,11 +496,8 @@
             pl.when(final)(lambda: relay_early(h))
 
         def after_f(h):
-            pl.when(h == 0)(lambda: forward(LEAD, 1, l, par))
-
             @pl.when(h == 1)
             def _():
-                relayout(Q, l + 1, NO)
                 forward(LEAD, 2, l, par)
                 forward(LEAD, 3, l, par)
                 shared(KV)

time: 420 us -> 414 us (0.986)
  Pallas kernels: 416 us -> 410 us
    pallas_call x1, Pallas kernels: 416 us -> 410 us  [body(): pl.pallas_call(functools.partial(_kernel, cp), out_shape=jax.ShapeDtypeSt...]
where the time goes in v5:
time: 414 us
  Pallas kernels  410 us (99%)
    pallas_call x1, Pallas kernels, body(): pl.pallas_call(functools.partial(_kernel, cp), out_shape=jax.ShapeDtypeSt...  410 us

profile of v5, /device:TPU:21, one launch (start us, length us, event | category | flops | bytes accessed | tf_op | source)
XLA Modules:
  0.0 413.7 jit_solution(5861846790156813705)
XLA Ops:
  0.0 410.2 %layers.1 = bf16[512,2560]{1,0:T(8,128)(2,1)} custom-call(bf16[512,2560]{1,0:T(8,128)(2,1)} %x_hbm.1, bf16[6,2560]{1,0:T(8,128)(2,1)} %g_ref.1, bf16[6,20480,256]{2,1,0:T(8,128)(2,1)} %bitcast.12, bf16[6,20480,128]{2,1,0:T(8,128)(2,1)} %bitcast.14, bf16[6,20480,128]{2,1,0:T(8,128)(2,1)} %bitcast.15, bf16[6,2048,2560]{2,1,0:T(8,128)(2,1)} %bitcast.13), custom_call_target="tpu_custom_call" | custom-call | tf_op jit(solution)/shard_map/layers/pallas_call | solution.py:660
  410.3 3.4 copy.10
